TPU v7x, 256 devices: a whole 4x4x8 slice. The times are simulated.
256 devices in a mesh: dp: 32 (over y, z), vocab: 8 (over x, core).
Axes of the slice: x: 4, y: 4, z: 8, core: 2. Of those that a mesh axis runs over, the one named last changes fastest.
Arguments:
- hidden_states: bfloat16 [16384, 2048], P('dp', 'vocab'), may hold values from -12 to 12
- teacher_logits: bfloat16 [16384, 16384], P('dp', 'vocab'), may hold values from -24 to 240
- head_weight: bfloat16 [2048, 16384], P(None, 'vocab'), as said below
Outputs:
- kl_per_token: float32 [16384], P('dp')
- hidden_grad: bfloat16 [16384, 2048], P('dp', 'vocab')
- head_grad: float32 [2048, 16384], P('dp', 'vocab')
Inputs may be any that keep to these rules, and one draw needn't show every extreme that they name: `head_weight`: every entry's magnitude is at most 18 / sqrt(2048).
All inputs are finite; a program needn't handle non-finite values.
Results may differ from a plain program's by a relative error of at most 0.014.
Values may be sent and summed in bfloat16 or wider, within the bound.
A program may use at most 128 MiB of HBM per device.

v0:
```python
import jax
import jax.numpy as jnp
from jax import lax
from jax.sharding import Mesh
from jax.sharding import PartitionSpec as P

MICRO = 2
DP = ("dp_0", "dp_1")


grad_scale = 8.0


def in_order(pieces, dim):
    lengths = list(pieces.shape[1:])
    lengths[dim] *= pieces.shape[0]
    return jnp.moveaxis(pieces, 0, dim).reshape(lengths)


def sent_to_all(array, axis):
    copies = jnp.broadcast_to(array, (lax.axis_size(axis), *array.shape))
    return lax.all_to_all(copies, axis, split_axis=0, concat_axis=0, tiled=True)


def gathered_copies(array, axis, dim):
    return in_order(sent_to_all(array, axis), dim)


def gathered_once(array, axis):
    leaves = jax.tree.leaves(array)
    turns = sorted(range(len(leaves)), key=lambda k: -leaves[k].size)
    width = (1, *leaves[turns[0]].shape)[-1]
    lines = [
        jnp.pad(leaves[k].reshape(-1), (0, -leaves[k].size % width)).reshape(-1, width)
        for k in turns
    ]
    both, at, found = (sent_to_all(jnp.concatenate(lines), axis), 0, {})
    for k, line in zip(turns, lines):
        share = both[:, at : at + len(line)].reshape(len(both), -1)
        found[k] = share[:, : leaves[k].size].reshape(-1, *leaves[k].shape)
        at += len(line)
    numbers = iter(range(len(leaves)))
    return jax.tree.map(lambda _: found[next(numbers)], array)


def folded_in_pairs(pieces, combine):
    while len(jax.tree.leaves(pieces)[0]) > 1:
        pieces = jax.vmap(combine)(
            *(jax.tree.map(lambda part: part[side::2], pieces) for side in (0, 1))
        )
    return jax.tree.map(lambda part: part[0], pieces)


def merged_2(array, axis, combine):
    pieces = gathered_once(array, axis)
    return folded_in_pairs(pieces, combine)


def in_blocks(array, dim, size):
    before, after = (array.shape[:dim], array.shape[dim + 1 :])
    return jnp.moveaxis(array.reshape(*before, size, -1, *after), dim, 0)


def summed_on_arrival(array, axis, dim):
    size = lax.axis_size(axis)
    pieces = lax.all_to_all(in_blocks(array, dim, size), axis, 0, 0, tiled=True)
    return jnp.sum(pieces.astype(jnp.float32), axis=0)


def sum_by_axis(array, axes, dim):
    if not axes:
        return array
    nearer = lax.psum_scatter(array, axes[0], scatter_dimension=dim, tiled=True)
    return sum_by_axis(nearer, axes[1:], dim)


def combine_rows(left_stats, right_stats):
    student_peak = jnp.maximum(left_stats[0], right_stats[0])
    left_scale = jnp.exp(left_stats[0] - student_peak)
    right_scale = jnp.exp(right_stats[0] - student_peak)
    student_total = left_stats[1] * left_scale + right_stats[1] * right_scale
    teacher_peak = jnp.maximum(left_stats[2], right_stats[2])
    left_weight = jnp.exp(left_stats[2] - teacher_peak)
    right_weight = jnp.exp(right_stats[2] - teacher_peak)
    teacher_total = left_stats[3] * left_weight + right_stats[3] * right_weight
    cross_term = left_stats[4] * left_weight + right_stats[4] * right_weight
    return (student_peak, student_total, teacher_peak, teacher_total, cross_term)


def micro_batch(hidden_part, teacher_part, head_weight):
    gathered = gathered_copies(hidden_part, "vocab", 1)
    student = jnp.dot(gathered, head_weight, preferred_element_type=jnp.float32)
    teacher = teacher_part.astype(jnp.float32)
    student_peak = jnp.max(student, axis=1)
    teacher_peak = jnp.max(teacher, axis=1)
    student_terms = jnp.exp(student - student_peak[:, None])
    teacher_terms = jnp.exp(teacher - teacher_peak[:, None])
    merged = merged_2(
        (
            student_peak,
            jnp.sum(student_terms, axis=1),
            teacher_peak,
            jnp.sum(teacher_terms, axis=1),
            jnp.sum(teacher_terms * (teacher - student), axis=1),
        ),
        "vocab",
        combine_rows,
    )
    student_max, student_total, teacher_max, teacher_total, cross_term = merged
    student_terms = student_terms * jnp.exp(student_peak - student_max)[:, None]
    teacher_terms = teacher_terms * jnp.exp(teacher_peak - teacher_max)[:, None]
    divergence = (
        cross_term / teacher_total
        - teacher_max
        - jnp.log(teacher_total)
        + student_max
        + jnp.log(student_total)
    )
    logit_grad = (
        grad_scale
        * (student_terms / student_total[:, None] - teacher_terms / teacher_total[:, None])
    ).astype(jnp.bfloat16)
    partial_value = lax.dot_general(
        logit_grad, head_weight, (((1,), (1,)), ((), ())), preferred_element_type=jnp.float32
    )
    hidden_grad = summed_on_arrival(partial_value.astype(jnp.bfloat16), "vocab", 1).astype(
        jnp.bfloat16
    )
    return (gathered, logit_grad, hidden_grad, divergence)


def per_device(hidden_states, teacher_logits, head_weight):
    device_rows = hidden_states.shape[0]
    micro_rows = device_rows // MICRO
    model_width = head_weight.shape[0]
    local_vocab = head_weight.shape[1]
    initial = jnp.zeros((model_width, local_vocab), jnp.float32)
    running = initial
    collected = []
    for number in range(MICRO):
        row_begin = number * micro_rows
        row_end = row_begin + micro_rows
        accumulate_running = running
        gathered, logit_grad, accumulate_hidden_grad, accumulate_divergence = micro_batch(
            hidden_states[row_begin:row_end], teacher_logits[row_begin:row_end], head_weight
        )
        accumulate_running = accumulate_running + lax.dot_general(
            gathered, logit_grad, (((0,), (0,)), ((), ())), preferred_element_type=jnp.float32
        )
        running = accumulate_running
        produced = (accumulate_hidden_grad, accumulate_divergence)
        collected.append(produced)
    results = tuple((jnp.concatenate(column, axis=0) for column in zip(*collected)))
    hidden_grad = results[0]
    divergence = results[1]
    head_grad = sum_by_axis(running.astype(jnp.bfloat16), DP, 0).astype(jnp.float32)
    return (divergence, hidden_grad, head_grad)


def solution(mesh):
    split = Mesh(mesh.devices.reshape(4, 8, mesh.shape["vocab"]), ("dp_0", "dp_1", "vocab"))
    placed = (P(DP, "vocab"), P(DP, "vocab"), P(None, "vocab"))
    return jax.shard_map(
        per_device,
        mesh=split,
        in_specs=placed,
        out_specs=(P(DP), P(DP, "vocab"), P(DP, "vocab")),
        check_vma=False,
    )
```

profile of v0, /device:TPU:2, one launch (start us, length us, event | category | flops | bytes accessed | tf_op | source)
XLA Modules:
  0.0 244.7 jit_solution(8956937565162320804)
XLA Ops:
  8.3 1.1 broadcast_in_dim.8
  9.3 5.7 %all-to-all-start = ((bf16[8,256,256]{1,2,0:T(8,128)(2,1)}), bf16[8,256,256]{1,2,0:T(8,128)(2,1)S(1)}, u32[]{:S(2)}, u32[]{:S(2)}) async-start(bf16[8,256,256]{1,2,0:T(8,128)(2,1)} %broadcast_in_dim.8), calls=%async_computation | async-start | bytes 2097152 | tf_op jit(solution)/shard_map/all_to_all | solution.py:22
  15.1 14.4 %all-to-all-done = bf16[8,256,256]{1,2,0:T(8,128)(2,1)S(1)} async-done(((bf16[8,256,256]{1,2,0:T(8,128)(2,1)}), bf16[8,256,256]{1,2,0:T(8,128)(2,1)S(1)}, u32[]{:S(2)}, u32[]{:S(2)}) %all-to-all-start) | async-done | bytes 1048608 | tf_op jit(solution)/shard_map/all_to_all | solution.py:22
  30.6 5.6 %all-to-all-start.2 = ((bf16[8,256,256]{1,2,0:T(8,128)(2,1)}), bf16[8,256,256]{1,2,0:T(8,128)(2,1)}, u32[]{:S(2)}, u32[]{:S(2)}) async-start(bf16[8,256,256]{1,2,0:T(8,128)(2,1)} %broadcast_in_dim.10), calls=%async_computation.2 | async-start | bytes 2097152 | tf_op jit(solution)/shard_map/all_to_all | solution.py:22
  36.5 7.1 %fusion.36 = (f32[256]{0:T(256)S(1)}, f32[256,2048]{1,0:T(8,128)}) fusion(bf16[256,2048]{0,1:T(8,128)(2,1)S(1)} %bitcast.81, bf16[2048,2048]{1,0:T(8,128)(2,1)} %param.5), kind=kOutput, calls=%fused_computation.103 | convolution fusion | flops 2148007680 | bytes 11535360 | tf_op jit(solution)/shard_map/dot_general | solution.py:92
  43.7 7.1 %all-to-all-done.2 = bf16[8,256,256]{1,2,0:T(8,128)(2,1)} async-done(((bf16[8,256,256]{1,2,0:T(8,128)(2,1)}), bf16[8,256,256]{1,2,0:T(8,128)(2,1)}, u32[]{:S(2)}, u32[]{:S(2)}) %all-to-all-start.2) | async-done | bytes 1048608 | tf_op jit(solution)/shard_map/all_to_all | solution.py:22
  50.8 6.3 %fusion.35 = (f32[256]{0:T(256)S(1)}, f32[256,2048]{1,0:T(8,128)S(1)}) fusion(bf16[256,2048]{0,1:T(8,128)(2,1)} %bitcast.16, bf16[2048,2048]{1,0:T(8,128)(2,1)} %param.5), kind=kOutput, calls=%fused_computation.102 | convolution fusion | flops 2148007680 | bytes 11535360 | tf_op jit(solution)/shard_map/dot_general | solution.py:92
  57.1 2.2 fusion.5
  60.0 4.7 %all-to-all-start.3 = ((f32[8,5,256]{2,1,0:T(8,128)}), f32[8,5,256]{2,1,0:T(8,128)S(1)}, u32[]{:S(2)}, u32[]{:S(2)}) async-start(f32[8,5,256]{2,1,0:T(8,128)} %broadcast_in_dim.11), calls=%async_computation.3 | async-start | bytes 131072 | tf_op jit(solution)/shard_map/all_to_all | solution.py:22
  64.7 4.2 %all-to-all-done.3 = f32[8,5,256]{2,1,0:T(8,128)S(1)} async-done(((f32[8,5,256]{2,1,0:T(8,128)}), f32[8,5,256]{2,1,0:T(8,128)S(1)}, u32[]{:S(2)}, u32[]{:S(2)}) %all-to-all-start.3) | async-done | bytes 40992 | tf_op jit(solution)/shard_map/all_to_all | solution.py:22
  69.5 4.7 %all-to-all-start.1 = ((f32[8,5,256]{2,1,0:T(8,128)}), f32[8,5,256]{2,1,0:T(8,128)S(1)}, u32[]{:S(2)}, u32[]{:S(2)}) async-start(f32[8,5,256]{2,1,0:T(8,128)} %broadcast_in_dim.9), calls=%async_computation.1 | async-start | bytes 131072 | tf_op jit(solution)/shard_map/all_to_all | solution.py:22
  74.8 3.6 %all-to-all-done.1 = f32[8,5,256]{2,1,0:T(8,128)S(1)} async-done(((f32[8,5,256]{2,1,0:T(8,128)}), f32[8,5,256]{2,1,0:T(8,128)S(1)}, u32[]{:S(2)}, u32[]{:S(2)}) %all-to-all-start.1) | async-done | bytes 40992 | tf_op jit(solution)/shard_map/all_to_all | solution.py:22
  79.2 10.6 %fusion.27 = f32[2048,2048]{1,0:T(8,128)} fusion(bf16[256,2048]{0,1:T(8,128)(2,1)S(1)} %bitcast.82, f32[256,2048]{1,0:T(8,128)} %get-tuple-element.67, f32[256]{0:T(256)S(1)} %bitcast.125, f32[256]{0:T(256)S(1)} %get-tuple-element.68, f32[256]{0:T(256)S(1)} %bitcast.128, f32[256]{0:T(256)S(1)} %get-tuple-element.70, f32[256]{0:T(256)S(1)} %reduce_max.64, ...), kind=kOutput, calls=%fused_computation.98 | convolution fusion | flops 2152726528 | bytes 20977664 | tf_op jit(solution)/shard_map/dot_general | solution.py:147
  89.9 9.9 %fusion = bf16[2048,2048]{0,1:T(8,128)(2,1)} fusion(f32[2048,2048]{1,0:T(8,128)} %fusion.27, bf16[256,2048]{0,1:T(8,128)(2,1)} %bitcast.16, f32[256,2048]{1,0:T(8,128)S(1)} %copy-done.3, f32[256]{0:T(256)S(1)} %bitcast.119, f32[256]{0:T(256)S(1)} %get-tuple-element.63, f32[256]{0:T(256)S(1)} %bitcast.122, f32[256]{0:T(256)S(1)} %get-tuple-element.61, ...), kind=kOutput, calls=%fused_computation.1 | convolution fusion | flops 2161115136 | bytes 29366272 | tf_op jit(solution)/shard_map/dot_general | solution.py:147
  99.8 84.3 %reduce-scatter.5.cloned.1.call-done = bf16[512,2048]{0,1:T(8,128)(2,1)} async-done(((bf16[2048,2048]{0,1:T(8,128)(2,1)}), bf16[512,2048]{0,1:T(8,128)(2,1)}) %reduce-scatter.5.cloned.1.call-update) | async-done | bytes 2097168 | tf_op jit(solution)/shard_map/reduce_scatter | solution.py:73
  184.1 4.0 %copy.33 = bf16[512,2048]{1,0:T(8,128)(2,1)} copy(bf16[512,2048]{0,1:T(8,128)(2,1)} %reduce-scatter.5.cloned.1.call-done) | data formatting | bytes 4194304
  188.1 6.9 %convolution_convert_fusion = bf16[256,2048]{1,0:T(8,128)(2,1)S(1)} fusion(bf16[2048,2048]{1,0:T(8,128)(2,1)} %param.5, f32[256,2048]{1,0:T(8,128)} %copy-done.2, f32[256]{0:T(256)S(1)} %bitcast.120, f32[256]{0:T(256)S(1)} %get-tuple-element.63, f32[256]{0:T(256)S(1)} %bitcast.123, f32[256]{0:T(256)S(1)} %get-tuple-element.61, f32[256]{0:T(256)S(1)} %reduce_max.65, ...), kind=kOutput, calls=%fused_computation.6 | convolution fusion | flops 2153250816 | bytes 12589056 | tf_op jit(solution)/shard_map/dot_general | solution.py:123
  195.0 1.1 copy.59
  196.1 4.8 %all-to-all-start.5 = ((bf16[8,256,256]{2,1,0:T(8,128)(2,1)}), bf16[8,256,256]{2,1,0:T(8,128)(2,1)S(1)}, u32[]{:S(2)}, u32[]{:S(2)}) async-start(bf16[8,256,256]{2,1,0:T(8,128)(2,1)} %bitcast.83), calls=%async_computation.5 | async-start | bytes 2097152 | tf_op jit(solution)/shard_map/all_to_all | solution.py:66
  200.9 6.9 %convolution_convert_fusion.1 = bf16[256,2048]{1,0:T(8,128)(2,1)S(1)} fusion(bf16[2048,2048]{1,0:T(8,128)(2,1)} %param.5, f32[256,2048]{1,0:T(8,128)} %get-tuple-element.67, f32[256]{0:T(256)S(1)} %bitcast.126, f32[256]{0:T(256)S(1)} %get-tuple-element.68, f32[256]{0:T(256)S(1)} %bitcast.129, f32[256]{0:T(256)S(1)} %get-tuple-element.70, ...), kind=kOutput, calls=%fused_computation.7 | convolution fusion | flops 2153250816 | bytes 12589056 | tf_op jit(solution)/shard_map/dot_general | solution.py:123
  208.8 6.5 %all-to-all-done.5 = bf16[8,256,256]{2,1,0:T(8,128)(2,1)S(1)} async-done(((bf16[8,256,256]{2,1,0:T(8,128)(2,1)}), bf16[8,256,256]{2,1,0:T(8,128)(2,1)S(1)}, u32[]{:S(2)}, u32[]{:S(2)}) %all-to-all-start.5) | async-done | bytes 1048608 | tf_op jit(solution)/shard_map/all_to_all | solution.py:66
  215.4 4.9 %all-to-all-start.4 = ((bf16[8,256,256]{2,1,0:T(8,128)(2,1)}), bf16[8,256,256]{2,1,0:T(8,128)(2,1)S(1)}, u32[]{:S(2)}, u32[]{:S(2)}) async-start(bf16[8,256,256]{2,1,0:T(8,128)(2,1)} %bitcast.70), calls=%async_computation.4 | async-start | bytes 2097152 | tf_op jit(solution)/shard_map/all_to_all | solution.py:66
  221.0 13.8 %all-to-all-done.4 = bf16[8,256,256]{2,1,0:T(8,128)(2,1)S(1)} async-done(((bf16[8,256,256]{2,1,0:T(8,128)(2,1)}), bf16[8,256,256]{2,1,0:T(8,128)(2,1)S(1)}, u32[]{:S(2)}, u32[]{:S(2)}) %all-to-all-start.4) | async-done | bytes 1048608 | tf_op jit(solution)/shard_map/all_to_all | solution.py:66
  235.7 1.2 copy.34
  (101 shorter events, 8.9 us)
Async XLA Ops:
  9.3 20.2 %all-to-all-start = ((bf16[8,256,256]{1,2,0:T(8,128)(2,1)}), bf16[8,256,256]{1,2,0:T(8,128)(2,1)S(1)}, u32[]{:S(2)}, u32[]{:S(2)}) async-start(bf16[8,256,256]{1,2,0:T(8,128)(2,1)} %broadcast_in_dim.8), calls=%async_computation | async-start | bytes 2097152 | tf_op jit(solution)/shard_map/all_to_all | solution.py:22
  15.0 21.1 %copy-start = (bf16[512,2048]{1,0:T(8,128)(2,1)S(1)}, bf16[512,2048]{1,0:T(8,128)(2,1)}, u32[]{:S(2)}) copy-start(bf16[512,2048]{1,0:T(8,128)(2,1)} %param.4) | copy-start | bytes 6291460
  30.6 20.2 %all-to-all-start.2 = ((bf16[8,256,256]{1,2,0:T(8,128)(2,1)}), bf16[8,256,256]{1,2,0:T(8,128)(2,1)}, u32[]{:S(2)}, u32[]{:S(2)}) async-start(bf16[8,256,256]{1,2,0:T(8,128)(2,1)} %broadcast_in_dim.10), calls=%async_computation.2 | async-start | bytes 2097152 | tf_op jit(solution)/shard_map/all_to_all | solution.py:22
  50.8 6.3 %copy-start.1 = (f32[256,2048]{1,0:T(8,128)S(1)}, f32[256,2048]{1,0:T(8,128)}, u32[]{:S(2)}) copy-start(f32[256,2048]{1,0:T(8,128)} %get-tuple-element.67) | copy-start | bytes 6291460
  57.1 2.2 copy-start.2
  60.0 8.9 %all-to-all-start.3 = ((f32[8,5,256]{2,1,0:T(8,128)}), f32[8,5,256]{2,1,0:T(8,128)S(1)}, u32[]{:S(2)}, u32[]{:S(2)}) async-start(f32[8,5,256]{2,1,0:T(8,128)} %broadcast_in_dim.11), calls=%async_computation.3 | async-start | bytes 131072 | tf_op jit(solution)/shard_map/all_to_all | solution.py:22
  69.5 8.9 %all-to-all-start.1 = ((f32[8,5,256]{2,1,0:T(8,128)}), f32[8,5,256]{2,1,0:T(8,128)S(1)}, u32[]{:S(2)}, u32[]{:S(2)}) async-start(f32[8,5,256]{2,1,0:T(8,128)} %broadcast_in_dim.9), calls=%async_computation.1 | async-start | bytes 131072 | tf_op jit(solution)/shard_map/all_to_all | solution.py:22
  74.2 109.9 %reduce-scatter.5.cloned.1.call-start = ((), (), s32[]{:S(2)}) async-start(), calls=%async_computation.8 | async-start | bytes 10485760 | tf_op jit(solution)/shard_map/reduce_scatter | solution.py:73
  79.2 10.6 %copy-start.3 = (f32[256,2048]{1,0:T(8,128)S(1)}, f32[256,2048]{1,0:T(8,128)}, u32[]{:S(2)}) copy-start(f32[256,2048]{1,0:T(8,128)} %copy-done.2) | copy-start | bytes 6291460
  99.8 135.9 %reduce-scatter.7.cloned.1.call-start = ((), (), s32[]{:S(2)}) async-start(), calls=%async_computation.9 | async-start | bytes 2359296
  196.1 19.3 %all-to-all-start.5 = ((bf16[8,256,256]{2,1,0:T(8,128)(2,1)}), bf16[8,256,256]{2,1,0:T(8,128)(2,1)S(1)}, u32[]{:S(2)}, u32[]{:S(2)}) async-start(bf16[8,256,256]{2,1,0:T(8,128)(2,1)} %bitcast.83), calls=%async_computation.5 | async-start | bytes 2097152 | tf_op jit(solution)/shard_map/all_to_all | solution.py:66
  215.4 19.4 %all-to-all-start.4 = ((bf16[8,256,256]{2,1,0:T(8,128)(2,1)}), bf16[8,256,256]{2,1,0:T(8,128)(2,1)S(1)}, u32[]{:S(2)}, u32[]{:S(2)}) async-start(bf16[8,256,256]{2,1,0:T(8,128)(2,1)} %bitcast.70), calls=%async_computation.4 | async-start | bytes 2097152 | tf_op jit(solution)/shard_map/all_to_all | solution.py:66
Sparse Core Ops, SparseCore 0:
  99.9 84.1 reduce-scatter.4
  188.2 42.1 reduce-scatter.6
where the time goes:
time: 247 us; the launch traced here: 245 us
  waiting for transfers between devices  134 us (54%)
  matrix products  47.7 us (19%)
  starting transfers between devices  30.5 us (12%)
  between operations  14.3 us (6%)
  local copies, waits for them, and re-layouts  13.9 us (6%)
  other arithmetic  4.43 us (2%)
    reduce_scatter x1, waiting for transfers between devices, sum_by_axis(): nearer = lax.psum_scatter(array, axes[0], scatter_dimension=dim, tiled=True)  84.3 us
    all_to_all x4, waiting for transfers between devices, sent_to_all(): return lax.all_to_all(copies, axis, split_axis=0, concat_axis=0, tiled=True)  29.3 us
    all_to_all x4, starting transfers between devices, sent_to_all(): return lax.all_to_all(copies, axis, split_axis=0, concat_axis=0, tiled=True)  20.7 us
    dot_general x2, matrix products, per_device(): lax.dot_general(gathered, logit_grad, (((0,), (0,)), ((), ())), preferred...  20.5 us
    all_to_all x2, waiting for transfers between devices, summed_on_arrival(): pieces = lax.all_to_all(in_blocks(array, dim, size), axis, 0, 0, tiled=True)  20.3 us
    dot_general x2, matrix products, micro_batch(): lax.dot_general(logit_grad, head_weight, (((1,), (1,)), ((), ())), prefer...  13.8 us
    dot_general x2, matrix products, micro_batch(): student = jnp.dot(gathered, head_weight, preferred_element_type=jnp.float32)  13.4 us
    all_to_all x2, starting transfers between devices, summed_on_arrival(): pieces = lax.all_to_all(in_blocks(array, dim, size), axis, 0, 0, tiled=True)  9.75 us
  transfers between devices with their start and end apart: 8, of which 7 were waited for; matrix products, arithmetic and copies ran while one was open for 10% of the time, Pallas kernels for 0%

commit v1 on v0

v1 whole, which is shorter than its diff:
```python
import jax
import jax.numpy as jnp
from jax import lax
from jax.experimental import pallas as pl
from jax.experimental.pallas import tpu as pltpu
from jax.sharding import Mesh
from jax.sharding import PartitionSpec as P

MESH = pl.DeviceIdType.MESH
F32, BF16 = jnp.float32, jnp.bfloat16
NY, NZ, NX = 4, 8, 4
ROWS, WIDTH, VOCAB, PART = 512, 2048, 2048, 256
GRAD_SCALE = 8.0
LANES = 128

A_WIDTH = 1152
A_SPLIT = (640, 512, 640, 512)
B_SUBS = ((1152, 512, 256), (1664, 384, 128))
A_PAIRS = ((4, 3), (5, 2), (6, 1), (7, 0))


def in_order(ops):
    rate = 46.0e3
    done, arrived, link_free, now, order = {}, {}, {}, 0.0, []
    left = list(ops)
    while left:
        best = None
        for rank, op in enumerate(left):
            if any(d not in done for d in op["after"]) or any(r not in arrived for r in op["recv"]):
                continue
            ready = max([now] + [arrived[r] for r in op["recv"]])
            key = (ready, op["rank"], rank)
            if best is None or key < best[0]:
                best = (key, op)
        (ready, _, _), op = best
        now = ready + op["time"]
        done[op["name"]] = now
        for link, size, key in op["send"]:
            begin = max(now, link_free.get(link, 0.0))
            wire = size / (rate if link != "c" else 600e3)
            link_free[link] = begin + wire
            arrived[key] = begin + wire + (2.0 if link != "c" else 1.0)
        order.append(op)
        left.remove(op)
    return order, now


def fold(op, tiles):
    tiles = list(tiles)
    while len(tiles) > 1:
        pairs = [op(a, b) for a, b in zip(tiles[::2], tiles[1::2])]
        tiles = pairs + ([tiles[-1]] if len(tiles) % 2 else [])
    return tiles[0]


def lane_tiles(value):
    return [value[:, i : i + LANES] for i in range(0, value.shape[1], LANES)]


def pieces(begin, width, step):
    return [(b, min(step, begin + width - b)) for b in range(begin, begin + width, step)]


SCRATCH = dict(
    hid=((8, ROWS, PART), BF16),
    hid_t=((NY, NZ, 64, ROWS), BF16),
    tea=((ROWS, VOCAB), BF16),
    head=((8, PART, VOCAB), BF16),
    stu=((ROWS, VOCAB), F32),
    stu_exp=((ROWS, VOCAB), F32),
    tea_exp=((ROWS, VOCAB), F32),
    grad=((ROWS, VOCAB), BF16),
    part_a=((ROWS, LANES), F32),
    part_b=((ROWS, LANES), F32),
    tea_max=((ROWS, LANES), F32),
    x_tea=((8, 8, LANES), F32),
    x_stu=((8, 8, LANES), F32),
    x_cross=((8, 8, LANES), F32),
    a1_s1=((2, 4, 128, 640), BF16),
    a1_r1=((2, 4, 128, 640), BF16),
    a1_s2=((2, 4, 128, A_WIDTH), BF16),
    a1_r2=((2, 4, 128, A_WIDTH), BF16),
    a1_sum=((8, 64, A_WIDTH), F32),
    a2_s1=((2, 64, 640), BF16),
    a2_r1=((2, 64, 640), BF16),
    a2_s=((2, 3, 64, A_WIDTH), BF16),
    a2_r=((2, 3, 64, A_WIDTH), BF16),
    b1_s1=((2, 2, 256, 256), BF16),
    b1_r1=((2, 2, 256, 256), BF16),
    b1_s=((2, 3, 256, VOCAB - A_WIDTH), BF16),
    b1_r=((2, 3, 256, VOCAB - A_WIDTH), BF16),
    b1_sum=((NY, 64, VOCAB - A_WIDTH), F32),
    b2_s1=((2, 2, 64, 256), BF16),
    b2_r1=((2, 2, 64, 256), BF16),
    b2_s2=((2, 64, VOCAB - A_WIDTH), BF16),
    b2_r2=((2, 64, VOCAB - A_WIDTH), BF16),
    hs_s=((4, ROWS, PART), BF16),
    hs_r=((4, ROWS, PART), BF16),
    h1_s=((2, 256, PART), BF16),
    h1_r=((2, 256, PART), BF16),
    h2_s=((2, ROWS, PART), BF16),
    h2_r=((2, ROWS, PART), BF16),
)
NAMES = tuple(SCRATCH)
N_COPIES = 120


def kernel(hidden_in, teacher_in, head_in, kl_out, hg_out, gh_out, *rest):
    bufs = dict(zip(NAMES, rest))
    load_sem, send_sem, recv_sem = rest[len(NAMES) :]
    hid, hid_t, tea, head, stu = (bufs[k] for k in ("hid", "hid_t", "tea", "head", "stu"))
    stu_exp, tea_exp, grad = bufs["stu_exp"], bufs["tea_exp"], bufs["grad"]
    part_a, part_b, tea_max = bufs["part_a"], bufs["part_b"], bufs["tea_max"]

    y, z, x, c = (lax.axis_index(a) for a in ("y", "z", "x", "c"))

    def near(axis, delta):
        here, size = {"y": (y, NY), "z": (z, NZ), "x": (x, NX)}[axis]
        return lax.rem(here + (delta % size), size)

    def vocab_at(dx, dc):
        return 2 * near("x", dx) + (c if dc == 0 else 1 - c)

    me, sib = vocab_at(0, 0), vocab_at(0, 1)
    to_sib = {"c": 1 - c}
    peers = [(dx, dc) for dx in range(NX) for dc in range(2) if (dx, dc) != (0, 0)]

    def peer(dx, dc):
        return {"x": near("x", dx), "c": c if dc == 0 else 1 - c}

    numbers, sent = {}, []

    def remote(key, src, dst, device):
        number = numbers.setdefault(key, len(numbers))
        assert number < N_COPIES
        return pltpu.make_async_remote_copy(
            src_ref=src,
            dst_ref=dst,
            send_sem=send_sem.at[number],
            recv_sem=recv_sem.at[number],
            device_id=device,
            device_id_type=MESH,
        )

    def send(key, src, dst, device):
        copy = remote(key, src, dst, device)
        copy.start()
        sent.append(copy)

    def arrive(key, dst, device=None):
        remote(key, dst, dst, to_sib).wait_recv()

    loads = [pltpu.make_async_copy(hidden_in, hid.at[me], load_sem.at[0])]
    loads[0].start()
    slots = [vocab_at(*p) for p in ((0, 0), (0, 1), (3, 0), (1, 0), (3, 1), (1, 1), (2, 0), (2, 1))]
    own, sibling, left, right, left_s, right_s, far, far_s = slots
    head_loads = []
    for k, slot in enumerate(slots):
        rows = pl.ds(pl.multiple_of(slot * PART, PART), PART)
        head_loads.append(pltpu.make_async_copy(head_in.at[rows], head.at[slot], load_sem.at[1 + k]))
    tea_load = pltpu.make_async_copy(teacher_in, tea, load_sem.at[9])
    head_loads[0].start()
    head_loads[1].start()
    tea_load.start()
    for copy in head_loads[2:]:
        copy.start()

    barrier = pltpu.get_barrier_semaphore()
    around = [peer(*p) for p in peers] + [{a: near(a, d)} for a in "yz" for d in (1, -1)]
    for device in around:
        pl.semaphore_signal(barrier, inc=1, device_id=device, device_id_type=MESH)
    pl.semaphore_wait(barrier, len(around))

    halves = (pl.ds(0, 256), pl.ds(256, 256))
    x_right, x_left = {"x": near("x", 1)}, {"x": near("x", -1)}
    loads[0].wait()

    def half(slot, h):
        return hid.at[slot, halves[h]]

    def give(key, slot, h, device):
        send(key, half(slot, h), half(slot, h), device)

    give("L0", own, 0, x_right)
    give("R1", own, 1, x_left)
    send("own", hid.at[own], hid.at[own], to_sib)
    give("L1", own, 1, x_right)
    give("R0", own, 0, x_left)

    waited = set()

    def logits(k, begin, rows):
        slot = slots[k]
        if k not in waited:
            head_loads[k].wait()
            waited.add(k)

        @pl.loop(0, VOCAB // 512)
        def _(n):
            cols = pl.ds(pl.multiple_of(n * 512, 512), 512)
            value = jnp.dot(
                hid[slot, begin : begin + rows, :], head[slot, :, cols], preferred_element_type=F32
            )
            if k == 0:
                stu[begin : begin + rows, cols] = value
            else:
                stu[begin : begin + rows, cols] += value

    def row_blocks(size, body):
        @pl.loop(0, ROWS // size)
        def _(n):
            body(pl.ds(pl.multiple_of(n * size, size), size))

    def spread_max(ref_in, ref_out):
        ref_out[...] = jnp.broadcast_to(jnp.max(ref_in[...], axis=1, keepdims=True), (ROWS, LANES))

    def tea_peaks(rows):
        part_a[rows, :] = fold(jnp.maximum, lane_tiles(tea[rows, :].astype(F32)))

    def tea_terms(rows):
        peak = tea_max[rows, :]
        total = None
        for i in range(0, VOCAB, LANES):
            term = jnp.exp(tea[rows, i : i + LANES].astype(F32) - peak)
            tea_exp[rows, i : i + LANES] = term
            total = term if total is None else total + term
        part_b[rows, :] = total

    def compact(ref, slot, at, peaks_ref):
        for b in range(4):
            rows = slice(b * LANES, (b + 1) * LANES)
            if peaks_ref is not None:
                ref[slot, b : b + 1, :] = peaks_ref[rows, :].T[0:1, :]
            ref[slot, at + b : at + b + 1, :] = jnp.sum(part_b[rows, :].T, axis=0, keepdims=True)

    def share(name):
        ref = bufs[name]
        for dx, dc in peers:
            send((name, dx, dc), ref.at[me], ref.at[me], peer(dx, dc))

    def shared(name):
        ref = bufs[name]
        for dx, dc in peers:
            slot = vocab_at(-dx, dc)
            arrive((name, dx, dc), ref.at[slot])

    def merged(ref):
        peak = fold(jnp.maximum, [ref[k, 0:4, :] for k in range(8)])
        total = None
        for k in range(8):
            term = ref[k, 4:8, :] * jnp.exp(ref[k, 0:4, :] - peak)
            total = term if total is None else total + term
        return peak, total

    def spread(value, ref):
        for b in range(4):
            ref[b * LANES : (b + 1) * LANES, :] = jnp.broadcast_to(
                value[b : b + 1, :], (LANES, LANES)
            ).T

    logits(0, 0, ROWS)
    arrive("own", hid.at[sibling])
    logits(1, 0, ROWS)
    tea_load.wait()
    row_blocks(32, tea_peaks)
    spread_max(part_a, tea_max)
    arrive("L0", half(left, 0))
    give("O0", left, 0, x_right)
    give("SL0", left, 0, to_sib)
    arrive("R1", half(right, 1))
    give("O1", right, 1, x_left)
    give("SR1", right, 1, to_sib)
    logits(2, 0, 256)
    logits(3, 256, 256)
    arrive("SL0", half(left_s, 0))
    logits(4, 0, 256)
    arrive("SR1", half(right_s, 1))
    logits(5, 256, 256)
    row_blocks(16, tea_terms)
    arrive("L1", half(left, 1))
    give("SL1", left, 1, to_sib)
    arrive("R0", half(right, 0))
    give("SR0", right, 0, to_sib)
    compact(bufs["x_tea"], me, 4, tea_max)
    share("x_tea")
    logits(2, 256, 256)
    logits(3, 0, 256)
    arrive("SL1", half(left_s, 1))
    logits(4, 256, 256)
    arrive("SR0", half(right_s, 0))
    logits(5, 0, 256)
    arrive("O0", half(far, 0))
    give("SO0", far, 0, to_sib)
    arrive("O1", half(far, 1))
    give("SO1", far, 1, to_sib)
    logits(6, 0, ROWS)
    arrive("SO0", half(far_s, 0))
    arrive("SO1", half(far_s, 1))
    logits(7, 0, ROWS)

    def stu_peaks(rows):
        part_a[rows, :] = fold(jnp.maximum, lane_tiles(stu[rows, :]))

    def stu_terms(rows):
        peak = part_a[rows, :]
        total = None
        for i in range(0, VOCAB, LANES):
            term = jnp.exp(stu[rows, i : i + LANES] - peak)
            stu_exp[rows, i : i + LANES] = term
            total = term if total is None else total + term
        part_b[rows, :] = total

    row_blocks(32, stu_peaks)
    spread_max(part_a, part_a)
    row_blocks(16, stu_terms)
    compact(bufs["x_stu"], me, 4, part_a)
    share("x_stu")

    for k in range(8):
        for b in range(4):
            rows = slice(b * LANES, (b + 1) * LANES)
            turned = hid[k, rows, :].T
            first = (k % 2) * 4
            hid_t[k // 2, first : first + 4, :, rows] = turned.reshape(4, 64, LANES)

    shared("x_tea")
    tea_peak, tea_total = merged(bufs["x_tea"])
    spread(GRAD_SCALE * jnp.exp(bufs["x_tea"][me, 0:4, :] - tea_peak) / tea_total, part_b)
    shared("x_stu")
    stu_peak, stu_total = merged(bufs["x_stu"])
    spread(GRAD_SCALE * jnp.exp(bufs["x_stu"][me, 0:4, :] - stu_peak) / stu_total, part_a)

    def grads(rows):
        stu_scale, tea_scale = part_a[rows, :], part_b[rows, :]
        for i in range(0, VOCAB, LANES):
            cols = slice(i, i + LANES)
            grad[rows, cols] = (stu_exp[rows, cols] * stu_scale - tea_exp[rows, cols] * tea_scale).astype(BF16)

    row_blocks(16, grads)

    ops = []

    def op(name, emit, time, rank, recv=(), send=(), after=()):
        ops.append(
            dict(name=name, emit=emit, time=time, rank=rank, recv=list(recv), send=list(send), after=list(after))
        )

    links = {("y", 0): "y+", ("y", 1): "y-", ("z", 0): "z+", ("z", 1): "z-", ("x", 0): "x+", ("x", 1): "x-"}

    def toward(axis, d):
        return {axis: near(axis, 1 if d == 0 else -1)}

    def signed(d, n):
        return n if d == 0 else -n

    def product(lhs, begin, width):
        return jnp.dot(lhs, grad[:, begin : begin + width], preferred_element_type=F32)

    def half_of(q_split, total, d):
        return (0, q_split) if d == 0 else (q_split, total - q_split)

    def a1_rows(q, dest):
        j = near("y", dest)
        return jnp.concatenate([hid_t[j, near("z", k)] for k in A_PAIRS[q]], axis=0)

    def a1_first(q, d):
        begin, width = half_of(A_SPLIT[q], A_WIDTH, d)
        src, dst = (bufs[n].at[d, q, :, pl.ds(0, width)] for n in ("a1_s1", "a1_r1"))

        def emit():
            lhs = a1_rows(q, 2)
            for b, w in pieces(0, width, 256):
                bufs["a1_s1"][d, q, :, b : b + w] = product(lhs, begin + b, w).astype(BF16)
            send(("a1", q, d, 1), src, dst, toward("y", d))

        op(("a1", q, d, 1), emit, 0.25, 1, send=[(links["y", d], 256 * width, ("a1", q, d, 1))])

    def a1_second(q, d):
        begin, width = half_of(A_SPLIT[q], A_WIDTH, d)

        def emit():
            arrive(("a1", q, d, 1), bufs["a1_r1"].at[d, q, :, pl.ds(0, width)])
            lhs = a1_rows(q, signed(d, 1))
            for b, w in pieces(0, begin, 256) + pieces(begin + width, A_WIDTH - begin - width, 256):
                bufs["a1_s2"][d, q, :, b : b + w] = product(lhs, b, w).astype(BF16)
            for b, w in pieces(begin, width, 256):
                got = bufs["a1_r1"][d, q, :, b - begin : b - begin + w].astype(F32)
                bufs["a1_s2"][d, q, :, b : b + w] = (product(lhs, b, w) + got).astype(BF16)
            send(("a1", q, d, 2), bufs["a1_s2"].at[d, q], bufs["a1_r2"].at[d, q], toward("y", d))

        op(
            ("a1", q, d, 2),
            emit,
            0.45,
            0,
            recv=[("a1", q, d, 1)],
            send=[(links["y", d], 256 * A_WIDTH, ("a1", q, d, 2))],
        )

    def a1_last(q):
        def emit():
            for d in range(2):
                arrive(("a1", q, d, 2), bufs["a1_r2"].at[d, q])
            lhs = a1_rows(q, 0)
            for b, w in pieces(0, A_WIDTH, 256):
                got = [bufs["a1_r2"][d, q, :, b : b + w].astype(F32) for d in range(2)]
                value = product(lhs, b, w) + got[0] + got[1]
                for i, k in enumerate(A_PAIRS[q]):
                    bufs["a1_sum"][k, :, b : b + w] = value[64 * i : 64 * (i + 1), :]

        op(("a1", q), emit, 0.5, 0, recv=[("a1", q, d, 2) for d in range(2)])

    for q in range(4):
        for d in range(2):
            a1_first(q, d)
            a1_second(q, d)
        a1_last(q)

    owner = {k: q for q, pair in enumerate(A_PAIRS) for k in pair}
    a2_split = 640

    def a2_step(d, step):
        begin, width = half_of(a2_split, A_WIDTH, d)
        dest = signed(d, 5 - step) % NZ
        if step == 1:
            src, dst = (bufs[n].at[d, :, pl.ds(0, width)] for n in ("a2_s1", "a2_r1"))
        else:
            src, dst = (bufs[n].at[d, step - 2] for n in ("a2_s", "a2_r"))

        def emit():
            total = bufs["a1_sum"]
            if step == 1:
                bufs["a2_s1"][d, :, 0:width] = total[dest, :, begin : begin + width].astype(BF16)
            elif step == 2:
                arrive(("a2", d, 1), bufs["a2_r1"].at[d, :, pl.ds(0, width)])
                bufs["a2_s"][d, 0] = total[dest].astype(BF16)
                got = bufs["a2_r1"][d, :, 0:width].astype(F32)
                bufs["a2_s"][d, 0, :, begin : begin + width] = (
                    total[dest, :, begin : begin + width] + got
                ).astype(BF16)
            else:
                arrive(("a2", d, step - 1), bufs["a2_r"].at[d, step - 3])
                got = bufs["a2_r"][d, step - 3].astype(F32)
                bufs["a2_s"][d, step - 2] = (total[dest] + got).astype(BF16)
            send(("a2", d, step), src, dst, toward("z", d))

        op(
            ("a2", d, step),
            emit,
            0.15,
            0,
            recv=[("a2", d, step - 1)] if step > 1 else [],
            send=[(links["z", d], 128 * (width if step == 1 else A_WIDTH), ("a2", d, step))],
            after=[("a1", owner[dest])],
        )

    def a2_last():
        def emit():
            for d in range(2):
                arrive(("a2", d, 4), bufs["a2_r"].at[d, 2])
            got = [bufs["a2_r"][d, 2].astype(F32) for d in range(2)]
            gh_out[:, 0:A_WIDTH] = bufs["a1_sum"][0] + got[0] + got[1]

        op("a2", emit, 0.15, 0, recv=[("a2", d, 4) for d in range(2)], after=[("a1", 3)])

    for d in range(2):
        for step in range(1, 5):
            a2_step(d, step)
    a2_last()

    def b1_rows(dest):
        return hid_t[:, near("z", dest)].reshape(256, ROWS)

    def b1_step(i, d, step):
        first, width, cut = B_SUBS[i]
        at = first - A_WIDTH
        begin, half_width = half_of(cut, width, d)
        dest = signed(d, 5 - step)
        cols = pl.ds(at, width)
        if step == 1:
            src, dst = (bufs[n].at[d, i, :, pl.ds(0, half_width)] for n in ("b1_s1", "b1_r1"))
        else:
            src, dst = (bufs[n].at[d, step - 2, :, cols] for n in ("b1_s", "b1_r"))

        def emit():
            lhs = b1_rows(dest)
            if step == 1:
                for b, w in pieces(0, half_width, 256):
                    bufs["b1_s1"][d, i, :, b : b + w] = product(lhs, first + begin + b, w).astype(BF16)
            elif step == 2:
                arrive(("b1", i, d, 1), bufs["b1_r1"].at[d, i, :, pl.ds(0, half_width)])
                for b, w in pieces(0, begin, 256) + pieces(begin + half_width, width - begin - half_width, 256):
                    bufs["b1_s"][d, 0, :, at + b : at + b + w] = product(lhs, first + b, w).astype(BF16)
                for b, w in pieces(begin, half_width, 256):
                    got = bufs["b1_r1"][d, i, :, b - begin : b - begin + w].astype(F32)
                    bufs["b1_s"][d, 0, :, at + b : at + b + w] = (product(lhs, first + b, w) + got).astype(BF16)
            else:
                arrive(("b1", i, d, step - 1), bufs["b1_r"].at[d, step - 3, :, cols])
                for b, w in pieces(0, width, 256):
                    got = bufs["b1_r"][d, step - 3, :, at + b : at + b + w].astype(F32)
                    bufs["b1_s"][d, step - 2, :, at + b : at + b + w] = (
                        product(lhs, first + b, w) + got
                    ).astype(BF16)
            send(("b1", i, d, step), src, dst, toward("z", d))

        op(
            ("b1", i, d, step),
            emit,
            0.3,
            0.5 if step > 1 else 0.9,
            recv=[("b1", i, d, step - 1)] if step > 1 else [],
            send=[(links["z", d], 512 * (half_width if step == 1 else width), ("b1", i, d, step))],
        )

    def b1_last(i):
        first, width, cut = B_SUBS[i]
        at = first - A_WIDTH

        def emit():
            for d in range(2):
                arrive(("b1", i, d, 4), bufs["b1_r"].at[d, 2, :, pl.ds(at, width)])
            lhs = b1_rows(0)
            for b, w in pieces(0, width, 256):
                got = [bufs["b1_r"][d, 2, :, at + b : at + b + w].astype(F32) for d in range(2)]
                value = product(lhs, first + b, w) + got[0] + got[1]
                bufs["b1_sum"][:, :, at + b : at + b + w] = value.reshape(NY, 64, w)

        op(("b1", i), emit, 0.4, 0, recv=[("b1", i, d, 4) for d in range(2)])

    def b2_step(i, d, step):
        first, width, cut = B_SUBS[i]
        at = first - A_WIDTH
        begin, half_width = half_of(cut, width, d)
        dest = signed(d, 3 - step)
        cols = pl.ds(at, width)
        if step == 1:
            src, dst = (bufs[n].at[d, i, :, pl.ds(0, half_width)] for n in ("b2_s1", "b2_r1"))
        else:
            src, dst = (bufs[n].at[d, :, cols] for n in ("b2_s2", "b2_r2"))

        def emit():
            j = near("y", dest)
            total = bufs["b1_sum"]
            mine = slice(at + begin, at + begin + half_width)
            if step == 1:
                bufs["b2_s1"][d, i, :, 0:half_width] = total[j, :, mine].astype(BF16)
            else:
                arrive(("b2", i, d, 1), bufs["b2_r1"].at[d, i, :, pl.ds(0, half_width)])
                bufs["b2_s2"][d, :, at : at + width] = total[j, :, at : at + width].astype(BF16)
                got = bufs["b2_r1"][d, i, :, 0:half_width].astype(F32)
                bufs["b2_s2"][d, :, mine] = (total[j, :, mine] + got).astype(BF16)
            send(("b2", i, d, step), src, dst, toward("y", d))

        op(
            ("b2", i, d, step),
            emit,
            0.1,
            0,
            recv=[("b2", i, d, 1)] if step > 1 else [],
            send=[(links["y", d], 128 * (half_width if step == 1 else width), ("b2", i, d, step))],
            after=[("b1", i)],
        )

    def b2_last(i):
        first, width, cut = B_SUBS[i]
        cols = slice(first - A_WIDTH, first - A_WIDTH + width)

        def emit():
            for d in range(2):
                arrive(("b2", i, d, 2), bufs["b2_r2"].at[d, :, pl.ds(first - A_WIDTH, width)])
            got = [bufs["b2_r2"][d, :, cols].astype(F32) for d in range(2)]
            gh_out[:, first : first + width] = bufs["b1_sum"][y, :, cols] + got[0] + got[1]

        op(("b2", i), emit, 0.1, 0, recv=[("b2", i, d, 2) for d in range(2)], after=[("b1", i)])

    for i in range(len(B_SUBS)):
        for d in range(2):
            for step in range(1, 5):
                b1_step(i, d, step)
        b1_last(i)
        for d in range(2):
            for step in (1, 2):
                b2_step(i, d, step)
        b2_last(i)

    hops = (2, 1, 3, 0)

    def back(slot, h):
        return lax.dot_general(
            grad[halves[h], :], head[slot], (((1,), (1,)), ((), ())), preferred_element_type=F32
        )

    def hs_step(n):
        def emit():
            slot = vocab_at(hops[n], 1)
            for h in range(2):
                bufs["hs_s"][n, halves[h], :] = back(slot, h).astype(BF16)
            send(("hs", n), bufs["hs_s"].at[n], bufs["hs_r"].at[n], to_sib)

        op(("hs", n), emit, 0.9, 3, send=[("c", 262144, ("hs", n))])

    def hg_step(n):
        def emit():
            arrive(("hs", n), bufs["hs_r"].at[n])
            if n == 1 or n == 2:
                d = n - 1
                arrive(("h1", d), bufs["h1_r"].at[d])
            if n == 3:
                for d in range(2):
                    arrive(("h2", d), bufs["h2_r"].at[d])
            slot = vocab_at(hops[n], 0)
            for h in range(2):
                rows = halves[h]
                value = back(slot, h) + bufs["hs_r"][n, rows, :].astype(F32)
                if n == 0:
                    bufs["h1_s"][h] = value.astype(BF16)
                    send(("h1", h), bufs["h1_s"].at[h], bufs["h1_r"].at[h], toward("x", h))
                elif n < 3:
                    if h == n - 1:
                        value = value + bufs["h1_r"][h].astype(F32)
                    bufs["h2_s"][n - 1, rows, :] = value.astype(BF16)
                else:
                    got = [bufs["h2_r"][d, rows, :].astype(F32) for d in range(2)]
                    hg_out[rows, :] = (value + got[0] + got[1]).astype(BF16)
            if n == 1 or n == 2:
                d = n - 1
                send(("h2", d), bufs["h2_s"].at[d], bufs["h2_r"].at[d], toward("x", d))

        recv = [("hs", n)] + {0: [], 1: [("h1", 0)], 2: [("h1", 1)], 3: [("h2", 0), ("h2", 1)]}[n]
        sends = {
            0: [("x+", 131072, ("h1", 0)), ("x-", 131072, ("h1", 1))],
            1: [("x+", 262144, ("h2", 0))],
            2: [("x-", 262144, ("h2", 1))],
            3: [],
        }[n]
        op(("hg", n), emit, 1.0, 3, recv=recv, send=sends)

    for n in range(4):
        hs_step(n)
        hg_step(n)

    def cross_share():
        def emit():
            def terms(rows):
                total = None
                for i in range(0, VOCAB, LANES):
                    cols = slice(i, i + LANES)
                    term = tea_exp[rows, cols] * (tea[rows, cols].astype(F32) - stu[rows, cols])
                    total = term if total is None else total + term
                part_b[rows, :] = total

            row_blocks(16, terms)
            ref = bufs["x_cross"]
            ref[me, 4:8, :] = jnp.zeros((4, LANES), F32)
            compact(ref, me, 0, None)
            share("x_cross")

        op("cross", emit, 1.5, 4)

    def divergence():
        def emit():
            shared("x_cross")
            ref, peaks = bufs["x_cross"], bufs["x_tea"]
            peak, total = merged(peaks)
            s_peak, s_total = merged(bufs["x_stu"])
            cross = None
            for k in range(8):
                term = ref[k, 0:4, :] * jnp.exp(peaks[k, 0:4, :] - peak)
                cross = term if cross is None else cross + term
            kl_out[...] = cross / total - peak - jnp.log(total) + s_peak + jnp.log(s_total)

        op("kl", emit, 0.3, 5, after=["cross", ("hg", 3)])

    cross_share()
    divergence()

    order, _ = in_order(ops)
    for step in order:
        step["emit"]()

    for copy in sent:
        copy.wait_send()


def per_device(hidden_states, teacher_logits, head_weight):
    vmem = pl.BlockSpec(memory_space=pltpu.VMEM)
    hbm = pl.BlockSpec(memory_space=pl.ANY)
    kl, hidden_grad, head_grad = pl.pallas_call(
        kernel,
        out_shape=(
            jax.ShapeDtypeStruct((4, LANES), F32),
            jax.ShapeDtypeStruct((ROWS, PART), BF16),
            jax.ShapeDtypeStruct((64, VOCAB), F32),
        ),
        in_specs=[hbm, hbm, hbm],
        out_specs=(vmem, vmem, vmem),
        scratch_shapes=[pltpu.VMEM(*SCRATCH[k]) for k in NAMES]
        + [
            pltpu.SemaphoreType.DMA((10,)),
            pltpu.SemaphoreType.DMA((N_COPIES,)),
            pltpu.SemaphoreType.DMA((N_COPIES,)),
        ],
        compiler_params=pltpu.CompilerParams(
            collective_id=0, has_side_effects=True, vmem_limit_bytes=66_000_000
        ),
    )(hidden_states, teacher_logits, head_weight)
    return kl.reshape(ROWS), hidden_grad, head_grad


def solution(mesh):
    split = Mesh(mesh.devices.reshape(NY, NZ, NX, 2), ("y", "z", "x", "c"))
    dp, vocab = ("y", "z"), ("x", "c")
    return jax.shard_map(
        per_device,
        mesh=split,
        in_specs=(P(dp, vocab), P(dp, vocab), P(None, vocab)),
        out_specs=(P(dp), P(dp, vocab), P(dp, vocab)),
        check_vma=False,
    )
```

time: 247 us -> 95.2 us (0.39)
  waiting for transfers between devices: 134 us -> 0 us
  Pallas kernels: 0 us -> 89.6 us
  matrix products: 47.7 us -> 0 us
  starting transfers between devices: 30.5 us -> 0 us
  between operations: 14.3 us -> 0.64 us
  local copies, waits for them, and re-layouts: 13.9 us -> 4.79 us
  other arithmetic: 4.43 us -> 0 us
    pallas_call x0 -> x1, Pallas kernels: none -> 89.6 us  [per_device(): pl.pallas_call(kernel, out_shape=(jax.ShapeDtypeStruct((4, LANES), F32),...]
    reduce_scatter x1 -> x0, waiting for transfers between devices: 84.3 us -> none  [sum_by_axis(): nearer = lax.psum_scatter(array, axes[0], scatter_dimension=dim, tiled=True)]
    all_to_all x6 -> x0, waiting for transfers between devices: 49.6 us -> none  [the longest x4 29.3 us: sent_to_all(): return lax.all_to_all(copies, axis, split_axis=0, concat_axis=0, tiled=True)]
    dot_general x6 -> x0, matrix products: 47.7 us -> none  [the longest x2 20.5 us: per_device(): lax.dot_general(gathered, logit_grad, (((0,), (0,)), ((), ())), preferred...]
    all_to_all x6 -> x0, starting transfers between devices: 30.5 us -> none  [the longest x4 20.7 us: sent_to_all(): return lax.all_to_all(copies, axis, split_axis=0, concat_axis=0, tiled=True)]
    broadcast_in_dim x4 -> x0, local copies, waits for them, and re-layouts: 3.37 us -> none  [sent_to_all(): copies = jnp.broadcast_to(array, (lax.axis_size(axis), *array.shape))]
    reduce_sum x3 -> x0, other arithmetic: 2.5 us -> none  [the longest x1 2.21 us: micro_batch(): jnp.sum(teacher_terms * (teacher - student), axis=1)]
    unnamed x21 -> x3, local copies, waits for them, and re-layouts: 6.21 us -> 4.79 us
  transfers between devices with their start and end apart: 8 -> 0, of which waited for: 7 -> 0; matrix products, arithmetic and copies ran while one was open for 10% -> 0% of each run, Pallas kernels for 0% -> 0%
where the time goes in v1:
time: 95.2 us; the launch traced here: 95 us
  Pallas kernels  89.6 us (94%)
  local copies, waits for them, and re-layouts  4.79 us (5%)
    pallas_call x1, Pallas kernels, per_device(): pl.pallas_call(kernel, out_shape=(jax.ShapeDtypeStruct((4, LANES), F32),...  89.6 us
    unnamed x3, local copies, waits for them, and re-layouts  4.79 us

profile of v1, /device:TPU:2, one launch (start us, length us, event | category | flops | bytes accessed | tf_op | source)
XLA Modules:
  0.0 95.0 jit_solution(3185641198296748267)
XLA Ops:
  0.6 89.6 %shard_map.58 = (f32[4,128]{1,0:T(4,128)}, bf16[512,256]{1,0:T(8,128)(2,1)}, f32[64,2048]{1,0:T(8,128)}) custom-call(bf16[512,256]{1,0:T(8,128)(2,1)} %hidden_in.1, bf16[512,2048]{1,0:T(8,128)(2,1)} %teacher_in.1, bf16[2048,2048]{1,0:T(8,128)(2,1)} %head_in.1), custom_call_target="tpu_custom_call" | custom-call | tf_op jit(solution)/shard_map/pallas_call | solution.py:688
  90.2 1.3 %copy.9 = f32[512]{0:T(512)} copy(f32[512]{0:T(512)} %bitcast.1) | data formatting | bytes 4096
  91.4 1.7 %copy.10 = bf16[512,256]{1,0:T(8,128)(2,1)} copy(bf16[512,256]{1,0:T(8,128)(2,1)} %get-tuple-element.13) | data formatting | bytes 524288
  93.1 1.9 %copy.11 = f32[64,2048]{1,0:T(8,128)} copy(f32[64,2048]{1,0:T(8,128)} %get-tuple-element.14) | data formatting | bytes 1048576

commit v2 on v1

--- a/solution.py
+++ b/solution.py
@@ -103,6 +103,7 @@
 )
 NAMES = tuple(SCRATCH)
 N_COPIES = 120
+LOAD_ORDER = (0, 3, 1, 2)
 
 
 def kernel(hidden_in, teacher_in, head_in, kl_out, hg_out, gh_out, *rest):
@@ -152,8 +153,8 @@
 
     loads = [pltpu.make_async_copy(hidden_in, hid.at[me], load_sem.at[0])]
     loads[0].start()
-    slots = [vocab_at(*p) for p in ((0, 0), (0, 1), (3, 0), (1, 0), (3, 1), (1, 1), (2, 0), (2, 1))]
-    own, sibling, left, right, left_s, right_s, far, far_s = slots
+    slots = [vocab_at(*p) for k in LOAD_ORDER for p in ((k, 0), (k, 1))]
+    own, sibling, left, left_s, right, right_s, far, far_s = slots
     head_loads = []
     for k, slot in enumerate(slots):
         rows = pl.ds(pl.multiple_of(slot * PART, PART), PART)
@@ -187,24 +188,21 @@
     give("L1", own, 1, x_right)
     give("R0", own, 0, x_left)
 
-    waited = set()
-
-    def logits(k, begin, rows):
-        slot = slots[k]
-        if k not in waited:
-            head_loads[k].wait()
-            waited.add(k)
+    def logits(k, first=False):
+        chip = near("x", k)
+        for n in range(2):
+            head_loads[2 * LOAD_ORDER.index(k) + n].wait()
 
         @pl.loop(0, VOCAB // 512)
         def _(n):
             cols = pl.ds(pl.multiple_of(n * 512, 512), 512)
-            value = jnp.dot(
-                hid[slot, begin : begin + rows, :], head[slot, :, cols], preferred_element_type=F32
-            )
-            if k == 0:
-                stu[begin : begin + rows, cols] = value
+            lhs = jnp.concatenate([hid[2 * chip], hid[2 * chip + 1]], axis=1)
+            rhs = head[pl.ds(2 * chip, 2), :, cols].reshape(2 * PART, 512)
+            value = jnp.dot(lhs, rhs, preferred_element_type=F32)
+            if first:
+                stu[:, cols] = value
             else:
-                stu[begin : begin + rows, cols] += value
+                stu[:, cols] += value
 
     def row_blocks(size, body):
         @pl.loop(0, ROWS // size)
@@ -258,9 +256,8 @@
                 value[b : b + 1, :], (LANES, LANES)
             ).T
 
-    logits(0, 0, ROWS)
     arrive("own", hid.at[sibling])
-    logits(1, 0, ROWS)
+    logits(0, first=True)
     tea_load.wait()
     row_blocks(32, tea_peaks)
     spread_max(part_a, tea_max)
@@ -270,12 +267,6 @@
     arrive("R1", half(right, 1))
     give("O1", right, 1, x_left)
     give("SR1", right, 1, to_sib)
-    logits(2, 0, 256)
-    logits(3, 256, 256)
-    arrive("SL0", half(left_s, 0))
-    logits(4, 0, 256)
-    arrive("SR1", half(right_s, 1))
-    logits(5, 256, 256)
     row_blocks(16, tea_terms)
     arrive("L1", half(left, 1))
     give("SL1", left, 1, to_sib)
@@ -283,20 +274,19 @@
     give("SR0", right, 0, to_sib)
     compact(bufs["x_tea"], me, 4, tea_max)
     share("x_tea")
-    logits(2, 256, 256)
-    logits(3, 0, 256)
+    arrive("SL0", half(left_s, 0))
     arrive("SL1", half(left_s, 1))
-    logits(4, 256, 256)
-    arrive("SR0", half(right_s, 0))
-    logits(5, 0, 256)
+    logits(3)
     arrive("O0", half(far, 0))
     give("SO0", far, 0, to_sib)
     arrive("O1", half(far, 1))
     give("SO1", far, 1, to_sib)
-    logits(6, 0, ROWS)
+    arrive("SR0", half(right_s, 0))
+    arrive("SR1", half(right_s, 1))
+    logits(1)
     arrive("SO0", half(far_s, 0))
     arrive("SO1", half(far_s, 1))
-    logits(7, 0, ROWS)
+    logits(2)
 
     def stu_peaks(rows):
         part_a[rows, :] = fold(jnp.maximum, lane_tiles(stu[rows, :]))
@@ -682,6 +672,11 @@
         copy.wait_send()
 
 
+def handed_on(*refs):
+    for src, dst in zip(refs[:3], refs[3:]):
+        dst[...] = src[...]
+
+
 def per_device(hidden_states, teacher_logits, head_weight):
     vmem = pl.BlockSpec(memory_space=pltpu.VMEM)
     hbm = pl.BlockSpec(memory_space=pl.ANY)
@@ -704,6 +699,12 @@
             collective_id=0, has_side_effects=True, vmem_limit_bytes=66_000_000
         ),
     )(hidden_states, teacher_logits, head_weight)
+    kl, hidden_grad, head_grad = pl.pallas_call(
+        handed_on,
+        out_shape=tuple(jax.ShapeDtypeStruct(v.shape, v.dtype) for v in (kl, hidden_grad, head_grad)),
+        in_specs=[vmem] * 3,
+        out_specs=(vmem,) * 3,
+    )(kl, hidden_grad, head_grad)
     return kl.reshape(ROWS), hidden_grad, head_grad
 
 

time: 95.2 us -> 90 us (0.945)
  local copies, waits for them, and re-layouts: 4.79 us -> 0 us
    unnamed x3 -> x0, local copies, waits for them, and re-layouts: 4.79 us -> none
    pallas_call x1, Pallas kernels: 89.6 us -> 87.2 us  [per_device(): pl.pallas_call(kernel, out_shape=(jax.ShapeDtypeStruct((4, LANES), F32),...]
    pallas_call x0 -> x1, Pallas kernels: none -> 2.03 us  [per_device(): pl.pallas_call(handed_on, out_shape=tuple((jax.ShapeDtypeStruct(v.shape,...]
where the time goes in v2:
time: 90 us; the launch traced here: 89.9 us
  Pallas kernels  89.2 us (99%)
    pallas_call x1, Pallas kernels, per_device(): pl.pallas_call(kernel, out_shape=(jax.ShapeDtypeStruct((4, LANES), F32),...  87.2 us
    pallas_call x1, Pallas kernels, per_device(): pl.pallas_call(handed_on, out_shape=tuple((jax.ShapeDtypeStruct(v.shape,...  2.03 us

profile of v2, /device:TPU:2, one launch (start us, length us, event | category | flops | bytes accessed | tf_op | source)
XLA Modules:
  0.0 89.9 jit_solution(8934220294043848045)
XLA Ops:
  0.6 87.2 %shard_map.58 = (f32[4,128]{1,0:T(4,128)}, bf16[512,256]{1,0:T(8,128)(2,1)}, f32[64,2048]{1,0:T(8,128)}) custom-call(bf16[512,256]{1,0:T(8,128)(2,1)} %hidden_in.1, bf16[512,2048]{1,0:T(8,128)(2,1)} %teacher_in.1, bf16[2048,2048]{1,0:T(8,128)(2,1)} %head_in.1), custom_call_target="tpu_custom_call" | custom-call | tf_op jit(solution)/shard_map/pallas_call | solution.py:683
  87.8 2.0 %shard_map.59 = (f32[4,128]{1,0:T(4,128)}, bf16[512,256]{1,0:T(8,128)(2,1)}, f32[64,2048]{1,0:T(8,128)}) custom-call(f32[4,128]{1,0:T(4,128)} %get-tuple-element.9.refs_0_, bf16[512,256]{1,0:T(8,128)(2,1)} %get-tuple-element.10.refs_1_, f32[64,2048]{1,0:T(8,128)} %get-tuple-element.11.refs_2_), custom_call_target="tpu_custom_call" | custom-call | tf_op jit(solution)/shard_map/pallas_call | solution.py:702

commit v3 on v2

v3 whole, which is shorter than its diff:
```python
import jax
import jax.numpy as jnp
from jax import lax
from jax.experimental import pallas as pl
from jax.experimental.pallas import tpu as pltpu
from jax.sharding import Mesh
from jax.sharding import PartitionSpec as P

MESH = pl.DeviceIdType.MESH
F32, BF16 = jnp.float32, jnp.bfloat16
NY, NZ, NX = 4, 8, 4
ROWS, WIDTH, VOCAB, PART = 512, 2048, 2048, 256
GRAD_SCALE = 8.0
LANES = 128

CHUNKS = tuple((k, 128) for k in "ZABaABBaAB")


def chunk_table():
    table, begin, half = [], 0, 0
    for kind, width in CHUNKS:
        paired = kind not in "Bb"
        table.append(dict(kind=kind.upper(), m=int(kind.islower()), w=width, paired=paired, at=begin, half=half))
        begin += width * (2 if paired else 1)
        half += width if paired else 0
    assert begin == VOCAB
    return table, half


TABLE, HALF_WIDTH = chunk_table()
EARLY = {("m", 0, "O"): 2.0, ("m", 1, "LR0"): 3.3, ("m", 1, "LR1"): 6.1}


def in_order(ops):
    rate = 46.0e3
    done, arrived, link_free, now, order = {}, dict(EARLY), {"x+": 2.9, "x-": 2.9}, 0.0, []
    left = list(ops)
    while left:
        best = None
        for rank, op in enumerate(left):
            if any(d not in done for d in op["after"]) or any(r not in arrived for r in op["recv"]):
                continue
            ready = max([now] + [arrived[r] for r in op["recv"]])
            key = (ready, op["rank"], rank)
            if best is None or key < best[0]:
                best = (key, op)
        (ready, _, _), op = best
        now = ready + op["time"]
        done[op["name"]] = now
        for link, size, key in op["send"]:
            begin = max(now, link_free.get(link, 0.0))
            wire = size / (rate if link != "c" else 600e3)
            link_free[link] = begin + wire
            arrived[key] = begin + wire + (2.8 if link != "c" else 1.0)
        order.append(op)
        left.remove(op)
    return order, now


def fold(op, tiles):
    tiles = list(tiles)
    while len(tiles) > 1:
        pairs = [op(a, b) for a, b in zip(tiles[::2], tiles[1::2])]
        tiles = pairs + ([tiles[-1]] if len(tiles) % 2 else [])
    return tiles[0]


def lane_tiles(value):
    return [value[:, i : i + LANES] for i in range(0, value.shape[1], LANES)]


SCRATCH = dict(
    hid=((8, ROWS, PART), BF16),
    hid_t=((3, NY, NZ, 64, ROWS), BF16),
    tea=((ROWS, VOCAB), BF16),
    head=((8, PART, VOCAB), BF16),
    stu=((ROWS, VOCAB), F32),
    stu_exp=((ROWS, VOCAB), F32),
    tea_exp=((ROWS, VOCAB), F32),
    grad=((ROWS, VOCAB), BF16),
    part_a=((ROWS, LANES), F32),
    part_b=((ROWS, LANES), F32),
    tea_max=((ROWS, LANES), F32),
    x_tea=((8, 8, LANES), F32),
    x_stu=((8, 8, LANES), F32),
    x_cross=((8, 8, LANES), F32),
    hid_m=((2, 8, ROWS, PART), BF16),
    grad_m=((ROWS, HALF_WIDTH), BF16),
    hs_s=((4, ROWS, PART), BF16),
    hs_r=((4, ROWS, PART), BF16),
    h1_s=((2, 256, PART), BF16),
    h1_r=((2, 256, PART), BF16),
    h2_s=((2, ROWS, PART), BF16),
    h2_r=((2, ROWS, PART), BF16),
)
for _i, _c in enumerate(TABLE):
    _w, _n = _c["w"], 2 if _c["kind"] == "A" else 4
    _cross = ROWS if _c["kind"] == "A" else 64
    for _side in "sr":
        SCRATCH[f"z1_{_side}{_i}"] = ((2, _n // 2, 64, _w), BF16)
        SCRATCH[f"z_{_side}{_i}"] = ((2, 3, _n, 64, _w), BF16)
        SCRATCH[f"x_{_side}{_i}"] = ((2, _cross, _w), BF16)
        SCRATCH[f"f_{_side}{_i}"] = ((64, _w), BF16)
    SCRATCH[f"z_sum{_i}"] = ((_n, 64, _w), F32)
    if _c["kind"] == "A":
        SCRATCH[f"a_sum{_i}"] = ((2, NZ, 64, _w), F32)
NAMES = tuple(SCRATCH)
N_COPIES = 200
WIDE = 1024


def kernel(hidden_in, teacher_in, head_in, kl_out, hg_out, gh_out, *rest):
    bufs = dict(zip(NAMES, rest))
    load_sem, send_sem, recv_sem = rest[len(NAMES) :]
    hid, hid_t, tea, head, stu = (bufs[k] for k in ("hid", "hid_t", "tea", "head", "stu"))
    stu_exp, tea_exp, grad = bufs["stu_exp"], bufs["tea_exp"], bufs["grad"]
    part_a, part_b, tea_max = bufs["part_a"], bufs["part_b"], bufs["tea_max"]

    y, z, x, c = (lax.axis_index(a) for a in ("y", "z", "x", "c"))

    def near(axis, delta):
        here, size = {"y": (y, NY), "z": (z, NZ), "x": (x, NX)}[axis]
        return lax.rem(here + (delta % size), size)

    def vocab_at(dx, dc):
        return 2 * near("x", dx) + (c if dc == 0 else 1 - c)

    me, sib = vocab_at(0, 0), vocab_at(0, 1)
    to_sib = {"c": 1 - c}
    peers = [(dx, dc) for dx in range(NX) for dc in range(2) if (dx, dc) != (0, 0)]

    def peer(dx, dc):
        return {"x": near("x", dx), "c": c if dc == 0 else 1 - c}

    numbers, sent = {}, []

    def remote(key, src, dst, device):
        number = numbers.setdefault(key, len(numbers))
        assert number < N_COPIES
        return pltpu.make_async_remote_copy(
            src_ref=src,
            dst_ref=dst,
            send_sem=send_sem.at[number],
            recv_sem=recv_sem.at[number],
            device_id=device,
            device_id_type=MESH,
        )

    def send(key, src, dst, device):
        copy = remote(key, src, dst, device)
        copy.start()
        sent.append(copy)

    def arrive(key, dst, device=None):
        remote(key, dst, dst, to_sib).wait_recv()

    loads = [pltpu.make_async_copy(hidden_in, hid.at[me], load_sem.at[0])]
    loads[0].start()
    slots = [vocab_at(*p) for p in ((0, 0), (0, 1), (3, 0), (1, 0), (3, 1), (1, 1), (2, 0), (2, 1))]
    own, sibling, left, right, left_s, right_s, far, far_s = slots
    head_loads = []
    for k, slot in enumerate(slots):
        rows = pl.ds(pl.multiple_of(slot * PART, PART), PART)
        head_loads.append(pltpu.make_async_copy(head_in.at[rows], head.at[slot], load_sem.at[1 + k]))
    tea_load = pltpu.make_async_copy(teacher_in, tea, load_sem.at[9])
    head_loads[0].start()
    head_loads[1].start()
    tea_load.start()
    for copy in head_loads[2:]:
        copy.start()

    barrier = pltpu.get_barrier_semaphore()
    around = [peer(*p) for p in peers] + [{a: near(a, d)} for a in "yz" for d in (1, -1)]
    for device in around:
        pl.semaphore_signal(barrier, inc=1, device_id=device, device_id_type=MESH)
    pl.semaphore_wait(barrier, len(around))

    halves = (pl.ds(0, 256), pl.ds(256, 256))
    x_right, x_left = {"x": near("x", 1)}, {"x": near("x", -1)}
    loads[0].wait()

    def half(slot, h):
        return hid.at[slot, halves[h]]

    def give(key, slot, h, device):
        send(key, half(slot, h), half(slot, h), device)

    give("L0", own, 0, x_right)
    give("R1", own, 1, x_left)
    send("own", hid.at[own], hid.at[own], to_sib)
    give("L1", own, 1, x_right)
    give("R0", own, 0, x_left)
    hid_m = bufs["hid_m"]
    rem2 = lax.rem(y, 2)
    partners = ({"y": y + 1 - 2 * rem2}, {"y": 3 - y})
    for m in range(2):
        send(("m", m, "y"), hid.at[own], hid_m.at[m, own], partners[m])

    def half_m(m, slot, h):
        return hid_m.at[m, slot, halves[h]]

    def give_m(m, key, slot, h, device):
        send(("m", m, key), half_m(m, slot, h), half_m(m, slot, h), device)

    def arrive_m(m, key, slot, h):
        arrive(("m", m, key), half_m(m, slot, h))

    def first_m(m):
        arrive(("m", m, "y"), hid_m.at[m, own])
        give_m(m, "L0", own, 0, x_right)
        give_m(m, "R1", own, 1, x_left)
        send(("m", m, "own"), hid_m.at[m, own], hid_m.at[m, own], to_sib)
        give_m(m, "L1", own, 1, x_right)
        give_m(m, "R0", own, 0, x_left)

    def second_m(m):
        arrive_m(m, "L0", left, 0)
        give_m(m, "O0", left, 0, x_right)
        give_m(m, "SL0", left, 0, to_sib)
        arrive_m(m, "R1", right, 1)
        give_m(m, "O1", right, 1, x_left)
        give_m(m, "SR1", right, 1, to_sib)

    def third_m(m):
        arrive_m(m, "L1", left, 1)
        give_m(m, "SL1", left, 1, to_sib)
        arrive_m(m, "R0", right, 0)
        give_m(m, "SR0", right, 0, to_sib)

    def fourth_m(m):
        for h in range(2):
            arrive_m(m, f"O{h}", far, h)
            give_m(m, f"SO{h}", far, h, to_sib)

    def turn(which, source):
        @pl.loop(0, NY)
        def _(j):
            for u in range(2):
                for b in range(4):
                    rows = slice(b * LANES, (b + 1) * LANES)
                    turned = source(2 * j + u, rows).T
                    hid_t[which, j, 4 * u : 4 * u + 4, :, rows] = turned.reshape(4, 64, LANES)

    def fifth_m(m):
        arrive(("m", m, "own"), hid_m.at[m, sibling])
        for h in range(2):
            arrive_m(m, f"SL{h}", left_s, h)
            arrive_m(m, f"SR{h}", right_s, h)
            arrive_m(m, f"SO{h}", far_s, h)
        turn(1 + m, lambda slot, rows: hid_m[m, slot, rows, :])

    def logits(ks, first=False):
        for k in ks:
            head_loads[k].wait()

        @pl.loop(0, VOCAB // WIDE)
        def _(n):
            cols = pl.ds(pl.multiple_of(n * WIDE, WIDE), WIDE)
            value = sum(
                jnp.dot(hid[slots[k]], head[slots[k], :, cols], preferred_element_type=F32) for k in ks
            )
            if first:
                stu[:, cols] = value
            else:
                stu[:, cols] += value

    def row_blocks(size, body):
        @pl.loop(0, ROWS // size)
        def _(n):
            body(pl.ds(pl.multiple_of(n * size, size), size))

    def spread_max(ref_in, ref_out):
        ref_out[...] = jnp.broadcast_to(jnp.max(ref_in[...], axis=1, keepdims=True), (ROWS, LANES))

    def tea_peaks(rows):
        part_a[rows, :] = fold(jnp.maximum, lane_tiles(tea[rows, :].astype(F32)))

    def tea_terms(rows):
        peak = tea_max[rows, :]
        total = None
        for i in range(0, VOCAB, LANES):
            term = jnp.exp(tea[rows, i : i + LANES].astype(F32) - peak)
            tea_exp[rows, i : i + LANES] = term
            total = term if total is None else total + term
        part_b[rows, :] = total

    def compact(ref, slot, at, peaks_ref):
        for b in range(4):
            rows = slice(b * LANES, (b + 1) * LANES)
            if peaks_ref is not None:
                ref[slot, b : b + 1, :] = peaks_ref[rows, :].T[0:1, :]
            ref[slot, at + b : at + b + 1, :] = jnp.sum(part_b[rows, :].T, axis=0, keepdims=True)

    def share(name):
        ref = bufs[name]
        for dx, dc in peers:
            send((name, dx, dc), ref.at[me], ref.at[me], peer(dx, dc))

    def shared(name):
        ref = bufs[name]
        for dx, dc in peers:
            slot = vocab_at(-dx, dc)
            arrive((name, dx, dc), ref.at[slot])

    def merged(ref):
        peak = fold(jnp.maximum, [ref[k, 0:4, :] for k in range(8)])
        total = None
        for k in range(8):
            term = ref[k, 4:8, :] * jnp.exp(ref[k, 0:4, :] - peak)
            total = term if total is None else total + term
        return peak, total

    def spread(value, ref):
        for b in range(4):
            ref[b * LANES : (b + 1) * LANES, :] = jnp.broadcast_to(
                value[b : b + 1, :], (LANES, LANES)
            ).T

    arrive("own", hid.at[sibling])
    logits((0, 1), first=True)
    tea_load.wait()
    row_blocks(32, tea_peaks)
    spread_max(part_a, tea_max)
    arrive("L0", half(left, 0))
    give("O0", left, 0, x_right)
    give("SL0", left, 0, to_sib)
    arrive("R1", half(right, 1))
    give("O1", right, 1, x_left)
    give("SR1", right, 1, to_sib)
    row_blocks(16, tea_terms)
    arrive("L1", half(left, 1))
    give("SL1", left, 1, to_sib)
    arrive("R0", half(right, 0))
    give("SR0", right, 0, to_sib)
    compact(bufs["x_tea"], me, 4, tea_max)
    share("x_tea")
    first_m(0)
    logits((2, 3))
    arrive("O0", half(far, 0))
    give("SO0", far, 0, to_sib)
    arrive("O1", half(far, 1))
    give("SO1", far, 1, to_sib)
    arrive("SL0", half(left_s, 0))
    arrive("SL1", half(left_s, 1))
    arrive("SR0", half(right_s, 0))
    arrive("SR1", half(right_s, 1))
    logits((4, 5))
    arrive("SO0", half(far_s, 0))
    arrive("SO1", half(far_s, 1))
    logits((6, 7))

    def stu_peaks(rows):
        part_a[rows, :] = fold(jnp.maximum, lane_tiles(stu[rows, :]))

    def stu_terms(rows):
        peak = part_a[rows, :]
        total = None
        for i in range(0, VOCAB, LANES):
            term = jnp.exp(stu[rows, i : i + LANES] - peak)
            stu_exp[rows, i : i + LANES] = term
            total = term if total is None else total + term
        part_b[rows, :] = total

    row_blocks(32, stu_peaks)
    spread_max(part_a, part_a)
    row_blocks(16, stu_terms)
    compact(bufs["x_stu"], me, 4, part_a)
    share("x_stu")

    turn(0, lambda slot, rows: hid[slot, rows, :])

    shared("x_tea")
    tea_peak, tea_total = merged(bufs["x_tea"])
    spread(GRAD_SCALE * jnp.exp(bufs["x_tea"][me, 0:4, :] - tea_peak) / tea_total, part_b)
    second_m(0)
    third_m(0)
    first_m(1)
    shared("x_stu")
    stu_peak, stu_total = merged(bufs["x_stu"])
    spread(GRAD_SCALE * jnp.exp(bufs["x_stu"][me, 0:4, :] - stu_peak) / stu_total, part_a)

    def grads(rows):
        stu_scale, tea_scale = part_a[rows, :], part_b[rows, :]
        for i in range(0, VOCAB, LANES):
            cols = slice(i, i + LANES)
            grad[rows, cols] = (stu_exp[rows, cols] * stu_scale - tea_exp[rows, cols] * tea_scale).astype(BF16)

    row_blocks(16, grads)

    ops = []

    def op(name, emit, time, rank, recv=(), send=(), after=()):
        ops.append(
            dict(name=name, emit=emit, time=time, rank=rank, recv=list(recv), send=list(send), after=list(after))
        )

    links = {("y", 0): "y+", ("y", 1): "y-", ("z", 0): "z+", ("z", 1): "z-", ("x", 0): "x+", ("x", 1): "x-"}

    def toward(axis, d):
        return {axis: near(axis, 1 if d == 0 else -1)}

    def signed(d, n):
        return n if d == 0 else -n

    grad_m = bufs["grad_m"]
    high = (y * (3 - y), y - rem2)

    op("g0o", lambda: fourth_m(0), 0.01, -3, recv=[("m", 0, "O")], send=[("c", 262144, ("m", 0, "SO"))])
    op("g0t", lambda: fifth_m(0), 0.78, -2, recv=[("m", 0, "SO")])
    op(
        "g1a",
        lambda: second_m(1),
        0.01,
        -3,
        recv=[("m", 1, "LR0")],
        send=[("x+", 131072, ("m", 1, "O0")), ("x-", 131072, ("m", 1, "O1")), ("c", 262144, ("m", 1, "S0"))],
    )
    op("g1b", lambda: third_m(1), 0.01, -3, recv=[("m", 1, "LR1")], send=[("c", 262144, ("m", 1, "S1"))], after=["g1a"])
    op(
        "g1o",
        lambda: fourth_m(1),
        0.01,
        -3,
        recv=[("m", 1, "O0"), ("m", 1, "O1")],
        send=[("c", 262144, ("m", 1, "SO"))],
        after=["g1b"],
    )
    op("g1t", lambda: fifth_m(1), 0.78, -2, recv=[("m", 1, k) for k in ("SO", "S0", "S1")])

    def chunk(i):
        info = TABLE[i]
        kind, m, w, paired, at, half_at = (info[k] for k in ("kind", "m", "w", "paired", "at", "half"))
        rank = 0.01 * i
        pair_link, cross_link = ("p", "q") if m == 0 else ("q", "p")
        partner, cross = partners[m], partners[1 - m]
        opposite = lax.rem(y + 2, NY)
        mine = pl.ds(pl.multiple_of(at + high[m] * (w // 2), LANES), w) if paired else pl.ds(at, w)
        theirs = pl.ds(pl.multiple_of(at + (2 - high[m]) * (w // 2), LANES), w) if paired else None
        got_cols = pl.ds(half_at, w)
        n = 2 if kind == "A" else 4
        z1_s, z1_r, z_s, z_r = (bufs[f"{k}{i}"] for k in ("z1_s", "z1_r", "z_s", "z_r"))
        x_s, x_r, f_s, f_r = (bufs[f"{k}{i}"] for k in ("x_s", "x_r", "f_s", "f_r"))
        z_sum = bufs[f"z_sum{i}"]

        def formed(rows_of):
            value = jnp.dot(rows_of(0), grad[:, mine], preferred_element_type=F32)
            if paired:
                value = value + jnp.dot(rows_of(1 + m), grad_m[:, got_cols], preferred_element_type=F32)
            return value

        def cost(rows):
            if kind == "A":
                return 0.71 if w == 128 else 1.1
            return ((0.3 if paired else 0.24) if rows == 256 else (0.22 if paired else 0.19)) * (1 if w == 128 else 1.5)

        start = []
        if paired:

            def emit_swap():
                send(("p", i), grad.at[:, theirs], grad_m.at[:, got_cols], partner)

            def emit_swapped():
                arrive(("p", i), grad_m.at[:, got_cols])

            op(("p", i), emit_swap, 0.02, -1 + rank, send=[(pair_link, 1024 * w, ("p", i))])
            op(("pr", i), emit_swapped, 0.01, rank, recv=[("p", i)], after=[f"g{m}t"])
            start = [("pr", i)]

        if kind == "A":
            a_sum = bufs[f"a_sum{i}"]

            def emit_cross():
                for u, j in enumerate((cross["y"], opposite)):
                    x_s[u] = formed(lambda t: hid_t[t, j].reshape(ROWS, ROWS)).astype(BF16)
                send(("q", i), x_s, x_r, cross)

            def emit_kept():
                arrive(("q", i), x_r)
                for u, j in enumerate((y, partner["y"])):
                    value = formed(lambda t: hid_t[t, j].reshape(ROWS, ROWS)) + x_r[u].astype(F32)
                    a_sum[u] = value.reshape(NZ, 64, w)

            op(("q", i), emit_cross, cost(1024), rank, send=[(cross_link, 2048 * w, ("q", i))], after=start)
            op(("qf", i), emit_kept, cost(1024), rank, recv=[("q", i)], after=start)
            start = [("qf", i)]

        def z_part(k, lo, count):
            if kind == "A":
                return a_sum[lo : lo + count, near("z", k)]
            value = formed(lambda t: hid_t[t, lo : lo + count, near("z", k)].reshape(64 * count, ROWS))
            return value.reshape(count, 64, w)

        h = n // 2

        def z_step(d, step):
            dest = signed(d, 5 - step)
            lo = d * h
            src, dst = (z1_s.at[d], z1_r.at[d]) if step == 1 else (z_s.at[d, step - 2], z_r.at[d, step - 2])

            def emit():
                if step == 1:
                    z1_s[d] = z_part(dest, lo, h).astype(BF16)
                elif step == 2:
                    arrive(("z", i, d, 1), z1_r.at[d])
                    z_s[d, 0, h - lo : n - lo] = z_part(dest, h - lo, h).astype(BF16)
                    z_s[d, 0, lo : lo + h] = (z_part(dest, lo, h) + z1_r[d].astype(F32)).astype(BF16)
                else:
                    arrive(("z", i, d, step - 1), z_r.at[d, step - 3])
                    z_s[d, step - 2] = (z_part(dest, 0, n) + z_r[d, step - 3].astype(F32)).astype(BF16)
                send(("z", i, d, step), src, dst, toward("z", d))

            time = 0.012 if kind == "A" else cost(128 if step == 1 else 256)
            op(
                ("z", i, d, step),
                emit,
                time,
                rank + (0.5 if step == 1 else 0),
                recv=[("z", i, d, step - 1)] if step > 1 else [],
                send=[(links["z", d], 128 * w * (h if step == 1 else n), ("z", i, d, step))],
                after=start,
            )

        def emit_z_last():
            for d in range(2):
                arrive(("z", i, d, 4), z_r.at[d, 2])
            z_sum[...] = z_part(0, 0, n) + z_r[0, 2].astype(F32) + z_r[1, 2].astype(F32)

        def finish(kept, other):
            f_s[...] = other.astype(BF16)
            send(("f", i), f_s, f_r, partner)
            if paired:
                gh_out[:, mine] = kept
            else:
                z_sum[0] = kept

        def emit_last():
            arrive(("f", i), f_r)
            if paired:
                gh_out[:, theirs] = f_r[...].astype(F32)
            else:
                gh_out[:, mine] = z_sum[0] + f_r[...].astype(F32)

        for d in range(2):
            for step in range(1, 5):
                z_step(d, step)
        op(("zf", i), emit_z_last, 0.012 if kind == "A" else cost(256), rank, recv=[("z", i, d, 4) for d in range(2)], after=start)
        final = [(pair_link, 128 * w, ("f", i))]
        if kind == "A":
            op(("fs", i), lambda: finish(z_sum[0], z_sum[1]), 0.02, rank, send=final, after=[("zf", i)])
            op(("ff", i), emit_last, 0.02, rank, recv=[("f", i)], after=[("fs", i)])
        else:

            def emit_cross_small():
                for u, j in enumerate((cross["y"], opposite)):
                    x_s[u] = z_sum[j].astype(BF16)
                send(("q", i), x_s, x_r, cross)

            def emit_kept_small():
                arrive(("q", i), x_r)
                finish(z_sum[y] + x_r[0].astype(F32), z_sum[partner["y"]] + x_r[1].astype(F32))

            op(("q", i), emit_cross_small, 0.02, rank, send=[(cross_link, 256 * w, ("q", i))], after=[("zf", i)])
            op(("qf", i), emit_kept_small, 0.02, rank, recv=[("q", i)], send=final, after=[("q", i)])
            op(("ff", i), emit_last, 0.02, rank, recv=[("f", i)], after=[("qf", i)])

    for i in range(len(TABLE)):
        chunk(i)

    hops = (2, 1, 3, 0)

    def back(slot, h):
        return lax.dot_general(
            grad[halves[h], :], head[slot], (((1,), (1,)), ((), ())), preferred_element_type=F32
        )

    def hs_step(n):
        def emit():
            slot = vocab_at(hops[n], 1)
            for h in range(2):
                bufs["hs_s"][n, halves[h], :] = back(slot, h).astype(BF16)
            send(("hs", n), bufs["hs_s"].at[n], bufs["hs_r"].at[n], to_sib)

        op(("hs", n), emit, 0.76, 3, send=[("c", 262144, ("hs", n))])

    def hg_step(n):
        def emit():
            arrive(("hs", n), bufs["hs_r"].at[n])
            if n == 1 or n == 2:
                d = n - 1
                arrive(("h1", d), bufs["h1_r"].at[d])
            if n == 3:
                for d in range(2):
                    arrive(("h2", d), bufs["h2_r"].at[d])
            slot = vocab_at(hops[n], 0)
            for h in range(2):
                rows = halves[h]
                value = back(slot, h) + bufs["hs_r"][n, rows, :].astype(F32)
                if n == 0:
                    bufs["h1_s"][h] = value.astype(BF16)
                    send(("h1", h), bufs["h1_s"].at[h], bufs["h1_r"].at[h], toward("x", h))
                elif n < 3:
                    if h == n - 1:
                        value = value + bufs["h1_r"][h].astype(F32)
                    bufs["h2_s"][n - 1, rows, :] = value.astype(BF16)
                else:
                    got = [bufs["h2_r"][d, rows, :].astype(F32) for d in range(2)]
                    hg_out[rows, :] = (value + got[0] + got[1]).astype(BF16)
            if n == 1 or n == 2:
                d = n - 1
                send(("h2", d), bufs["h2_s"].at[d], bufs["h2_r"].at[d], toward("x", d))

        recv = [("hs", n)] + {0: [], 1: [("h1", 0)], 2: [("h1", 1)], 3: [("h2", 0), ("h2", 1)]}[n]
        sends = {
            0: [("x+", 131072, ("h1", 0)), ("x-", 131072, ("h1", 1))],
            1: [("x+", 262144, ("h2", 0))],
            2: [("x-", 262144, ("h2", 1))],
            3: [],
        }[n]
        op(("hg", n), emit, 0.77 if n else 1.45, 3, recv=recv, send=sends)

    for n in range(4):
        hs_step(n)
        hg_step(n)

    def cross_share():
        def emit():
            def terms(rows):
                total = None
                for i in range(0, VOCAB, LANES):
                    cols = slice(i, i + LANES)
                    term = tea_exp[rows, cols] * (tea[rows, cols].astype(F32) - stu[rows, cols])
                    total = term if total is None else total + term
                part_b[rows, :] = total

            row_blocks(16, terms)
            ref = bufs["x_cross"]
            ref[me, 4:8, :] = jnp.zeros((4, LANES), F32)
            compact(ref, me, 0, None)
            share("x_cross")

        op("cross", emit, 1.06, 4)

    def divergence():
        def emit():
            shared("x_cross")
            ref, peaks = bufs["x_cross"], bufs["x_tea"]
            peak, total = merged(peaks)
            s_peak, s_total = merged(bufs["x_stu"])
            cross = None
            for k in range(8):
                term = ref[k, 0:4, :] * jnp.exp(peaks[k, 0:4, :] - peak)
                cross = term if cross is None else cross + term
            kl_out[...] = cross / total - peak - jnp.log(total) + s_peak + jnp.log(s_total)

        op("kl", emit, 0.05, 5, after=["cross", ("hg", 3)])

    cross_share()
    divergence()

    order, _ = in_order(ops)
    for step in order:
        step["emit"]()

    for copy in sent:
        copy.wait_send()


def handed_on(*refs):
    for src, dst in zip(refs[:3], refs[3:]):
        dst[...] = src[...]


def per_device(hidden_states, teacher_logits, head_weight):
    vmem = pl.BlockSpec(memory_space=pltpu.VMEM)
    hbm = pl.BlockSpec(memory_space=pl.ANY)
    kl, hidden_grad, head_grad = pl.pallas_call(
        kernel,
        out_shape=(
            jax.ShapeDtypeStruct((4, LANES), F32),
            jax.ShapeDtypeStruct((ROWS, PART), BF16),
            jax.ShapeDtypeStruct((64, VOCAB), F32),
        ),
        in_specs=[hbm, hbm, hbm],
        out_specs=(vmem, vmem, vmem),
        scratch_shapes=[pltpu.VMEM(*SCRATCH[k]) for k in NAMES]
        + [
            pltpu.SemaphoreType.DMA((10,)),
            pltpu.SemaphoreType.DMA((N_COPIES,)),
            pltpu.SemaphoreType.DMA((N_COPIES,)),
        ],
        compiler_params=pltpu.CompilerParams(
            collective_id=0, has_side_effects=True, vmem_limit_bytes=66_000_000
        ),
    )(hidden_states, teacher_logits, head_weight)
    kl, hidden_grad, head_grad = pl.pallas_call(
        handed_on,
        out_shape=tuple(jax.ShapeDtypeStruct(v.shape, v.dtype) for v in (kl, hidden_grad, head_grad)),
        in_specs=[vmem] * 3,
        out_specs=(vmem,) * 3,
    )(kl, hidden_grad, head_grad)
    return kl.reshape(ROWS), hidden_grad, head_grad


def solution(mesh):
    split = Mesh(mesh.devices.reshape(NY, NZ, NX, 2), ("y", "z", "x", "c"))
    dp, vocab = ("y", "z"), ("x", "c")
    return jax.shard_map(
        per_device,
        mesh=split,
        in_specs=(P(dp, vocab), P(dp, vocab), P(None, vocab)),
        out_specs=(P(dp), P(dp, vocab), P(dp, vocab)),
        check_vma=False,
    )
```

time: 90 us -> 85.5 us (0.950); the launches traced: 89.9 us -> 84 us
  Pallas kernels: 89.2 us -> 83.4 us
    pallas_call x1, Pallas kernels: 87.2 us -> 81.4 us  [per_device(): pl.pallas_call(kernel, out_shape=(jax.ShapeDtypeStruct((4, LANES), F32),...]
where the time goes in v3:
time: 85.5 us; the launch traced here: 84 us
  Pallas kernels  83.4 us (98%)
    pallas_call x1, Pallas kernels, per_device(): pl.pallas_call(kernel, out_shape=(jax.ShapeDtypeStruct((4, LANES), F32),...  81.4 us
    pallas_call x1, Pallas kernels, per_device(): pl.pallas_call(handed_on, out_shape=tuple((jax.ShapeDtypeStruct(v.shape,...  2.03 us

profile of v3, /device:TPU:2, one launch (start us, length us, event | category | flops | bytes accessed | tf_op | source)
XLA Modules:
  0.0 84.0 jit_solution(11113406023465710393)
XLA Ops:
  0.6 81.4 %shard_map.58 = (f32[4,128]{1,0:T(4,128)}, bf16[512,256]{1,0:T(8,128)(2,1)}, f32[64,2048]{1,0:T(8,128)}) custom-call(bf16[512,256]{1,0:T(8,128)(2,1)} %hidden_in.1, bf16[512,2048]{1,0:T(8,128)(2,1)} %teacher_in.1, bf16[2048,2048]{1,0:T(8,128)(2,1)} %head_in.1), custom_call_target="tpu_custom_call" | custom-call | tf_op jit(solution)/shard_map/pallas_call | solution.py:676
  82.0 2.0 %shard_map.59 = (f32[4,128]{1,0:T(4,128)}, bf16[512,256]{1,0:T(8,128)(2,1)}, f32[64,2048]{1,0:T(8,128)}) custom-call(f32[4,128]{1,0:T(4,128)} %get-tuple-element.9.refs_0_, bf16[512,256]{1,0:T(8,128)(2,1)} %get-tuple-element.10.refs_1_, f32[64,2048]{1,0:T(8,128)} %get-tuple-element.11.refs_2_), custom_call_target="tpu_custom_call" | custom-call | tf_op jit(solution)/shard_map/pallas_call | solution.py:695

commit v4 on v3

--- a/solution.py
+++ b/solution.py
@@ -13,14 +13,17 @@
 GRAD_SCALE = 8.0
 LANES = 128
 
-CHUNKS = tuple((k, 128) for k in "ZABaABBaAB")
+CHUNKS = tuple((k, 128) for k in "ZAabAbbbAa")
+RANKS = (0.8, 6.2, 8.9, 2.0, 9.1, 6.0, 6.7, 2.5, 8.9, 6.5)
+SWAPS = (1, 2, 9, 3, 7, 6, 5, 4, 0, 8)
+FIRST = -3
 
 
 def chunk_table():
     table, begin, half = [], 0, 0
-    for kind, width in CHUNKS:
+    for (kind, width), rank, turn in zip(CHUNKS, RANKS, SWAPS):
         paired = kind not in "Bb"
-        table.append(dict(kind=kind.upper(), m=int(kind.islower()), w=width, paired=paired, at=begin, half=half))
+        table.append(dict(kind=kind.upper(), m=int(kind.islower()), w=width, paired=paired, at=begin, half=half, rank=rank, turn=turn))
         begin += width * (2 if paired else 1)
         half += width if paired else 0
     assert begin == VOCAB
@@ -31,8 +34,10 @@
 EARLY = {("m", 0, "O"): 2.0, ("m", 1, "LR0"): 3.3, ("m", 1, "LR1"): 6.1}
 
 
+RATE = 46.0e3
+
+
 def in_order(ops):
-    rate = 46.0e3
     done, arrived, link_free, now, order = {}, dict(EARLY), {"x+": 2.9, "x-": 2.9}, 0.0, []
     left = list(ops)
     while left:
@@ -49,9 +54,10 @@
         done[op["name"]] = now
         for link, size, key in op["send"]:
             begin = max(now, link_free.get(link, 0.0))
-            wire = size / (rate if link != "c" else 600e3)
+            wire = size / (RATE if link != "c" else 600e3)
             link_free[link] = begin + wire
-            arrived[key] = begin + wire + (2.8 if link != "c" else 1.0)
+            hops = 0.75 if link[0] == "z" and key[0] == "f" or link[0] in "pq" and key[0] == "f" and key[2] == 2 else 0.0
+            arrived[key] = begin + wire + (2.8 + hops if link != "c" else 1.0)
         order.append(op)
         left.remove(op)
     return order, now
@@ -80,6 +86,7 @@
     grad=((ROWS, VOCAB), BF16),
     part_a=((ROWS, LANES), F32),
     part_b=((ROWS, LANES), F32),
+    part_c=((ROWS, LANES), F32),
     tea_max=((ROWS, LANES), F32),
     x_tea=((8, 8, LANES), F32),
     x_stu=((8, 8, LANES), F32),
@@ -95,17 +102,18 @@
 )
 for _i, _c in enumerate(TABLE):
     _w, _n = _c["w"], 2 if _c["kind"] == "A" else 4
-    _cross = ROWS if _c["kind"] == "A" else 64
     for _side in "sr":
         SCRATCH[f"z1_{_side}{_i}"] = ((2, _n // 2, 64, _w), BF16)
         SCRATCH[f"z_{_side}{_i}"] = ((2, 3, _n, 64, _w), BF16)
-        SCRATCH[f"x_{_side}{_i}"] = ((2, _cross, _w), BF16)
-        SCRATCH[f"f_{_side}{_i}"] = ((64, _w), BF16)
-    SCRATCH[f"z_sum{_i}"] = ((_n, 64, _w), F32)
+        SCRATCH[f"f_{_side}{_i}"] = ((3, 64, _w), BF16)
+        if _c["kind"] == "A":
+            SCRATCH[f"x_{_side}{_i}"] = ((2, ROWS, _w), BF16)
     if _c["kind"] == "A":
         SCRATCH[f"a_sum{_i}"] = ((2, NZ, 64, _w), F32)
+    else:
+        SCRATCH[f"z_sum{_i}"] = ((4, 64, _w), F32)
 NAMES = tuple(SCRATCH)
-N_COPIES = 200
+N_COPIES = 230
 WIDE = 1024
 
 
@@ -170,7 +178,8 @@
         copy.start()
 
     barrier = pltpu.get_barrier_semaphore()
-    around = [peer(*p) for p in peers] + [{a: near(a, d)} for a in "yz" for d in (1, -1)]
+    around = [peer(*p) for p in peers] + [{"y": near("y", d)} for d in (1, -1, 2)] + [{"z": near("z", d)} for d in (1, -1)]
+    around += [{"y": near("y", d), "z": near("z", e)} for d in (1, -1) for e in (1, -1)]
     for device in around:
         pl.semaphore_signal(barrier, inc=1, device_id=device, device_id_type=MESH)
     pl.semaphore_wait(barrier, len(around))
@@ -284,12 +293,12 @@
             total = term if total is None else total + term
         part_b[rows, :] = total
 
-    def compact(ref, slot, at, peaks_ref):
+    def compact(ref, slot, at, peaks_ref, sums_ref=part_b):
         for b in range(4):
             rows = slice(b * LANES, (b + 1) * LANES)
             if peaks_ref is not None:
                 ref[slot, b : b + 1, :] = peaks_ref[rows, :].T[0:1, :]
-            ref[slot, at + b : at + b + 1, :] = jnp.sum(part_b[rows, :].T, axis=0, keepdims=True)
+            ref[slot, at + b : at + b + 1, :] = jnp.sum(sums_ref[rows, :].T, axis=0, keepdims=True)
 
     def share(name):
         ref = bufs[name]
@@ -336,18 +345,19 @@
     share("x_tea")
     first_m(0)
     logits((2, 3))
-    arrive("O0", half(far, 0))
-    give("SO0", far, 0, to_sib)
-    arrive("O1", half(far, 1))
-    give("SO1", far, 1, to_sib)
     arrive("SL0", half(left_s, 0))
     arrive("SL1", half(left_s, 1))
     arrive("SR0", half(right_s, 0))
     arrive("SR1", half(right_s, 1))
     logits((4, 5))
+    arrive("O0", half(far, 0))
+    give("SO0", far, 0, to_sib)
+    arrive("O1", half(far, 1))
+    give("SO1", far, 1, to_sib)
+    logits((6,))
     arrive("SO0", half(far_s, 0))
     arrive("SO1", half(far_s, 1))
-    logits((6, 7))
+    logits((7,))
 
     def stu_peaks(rows):
         part_a[rows, :] = fold(jnp.maximum, lane_tiles(stu[rows, :]))
@@ -361,6 +371,14 @@
             total = term if total is None else total + term
         part_b[rows, :] = total
 
+    def cross_terms(rows):
+        total = None
+        for i in range(0, VOCAB, LANES):
+            cols = slice(i, i + LANES)
+            term = tea_exp[rows, cols] * (tea[rows, cols].astype(F32) - stu[rows, cols])
+            total = term if total is None else total + term
+        bufs["part_c"][rows, :] = total
+
     row_blocks(32, stu_peaks)
     spread_max(part_a, part_a)
     row_blocks(16, stu_terms)
@@ -375,6 +393,10 @@
     second_m(0)
     third_m(0)
     first_m(1)
+    row_blocks(16, cross_terms)
+    bufs["x_cross"][me, 4:8, :] = jnp.zeros((4, LANES), F32)
+    compact(bufs["x_cross"], me, 0, None, bufs["part_c"])
+    share("x_cross")
     shared("x_stu")
     stu_peak, stu_total = merged(bufs["x_stu"])
     spread(GRAD_SCALE * jnp.exp(bufs["x_stu"][me, 0:4, :] - stu_peak) / stu_total, part_a)
@@ -405,8 +427,8 @@
     grad_m = bufs["grad_m"]
     high = (y * (3 - y), y - rem2)
 
-    op("g0o", lambda: fourth_m(0), 0.01, -3, recv=[("m", 0, "O")], send=[("c", 262144, ("m", 0, "SO"))])
-    op("g0t", lambda: fifth_m(0), 0.78, -2, recv=[("m", 0, "SO")])
+    op("g0o", lambda: fourth_m(0), 0.01, -5, recv=[("m", 0, "O")], send=[("c", 262144, ("m", 0, "SO"))])
+    op("g0t", lambda: fifth_m(0), 0.78, -5, recv=[("m", 0, "SO")])
     op(
         "g1a",
         lambda: second_m(1),
@@ -425,12 +447,12 @@
         send=[("c", 262144, ("m", 1, "SO"))],
         after=["g1b"],
     )
-    op("g1t", lambda: fifth_m(1), 0.78, -2, recv=[("m", 1, k) for k in ("SO", "S0", "S1")])
+    op("g1t", lambda: fifth_m(1), 0.78, -5, recv=[("m", 1, k) for k in ("SO", "S0", "S1")])
 
     def chunk(i):
         info = TABLE[i]
         kind, m, w, paired, at, half_at = (info[k] for k in ("kind", "m", "w", "paired", "at", "half"))
-        rank = 0.01 * i
+        rank = info["rank"]
         pair_link, cross_link = ("p", "q") if m == 0 else ("q", "p")
         partner, cross = partners[m], partners[1 - m]
         opposite = lax.rem(y + 2, NY)
@@ -439,8 +461,7 @@
         got_cols = pl.ds(half_at, w)
         n = 2 if kind == "A" else 4
         z1_s, z1_r, z_s, z_r = (bufs[f"{k}{i}"] for k in ("z1_s", "z1_r", "z_s", "z_r"))
-        x_s, x_r, f_s, f_r = (bufs[f"{k}{i}"] for k in ("x_s", "x_r", "f_s", "f_r"))
-        z_sum = bufs[f"z_sum{i}"]
+        f_s, f_r = (bufs[f"{k}{i}"] for k in ("f_s", "f_r"))
 
         def formed(rows_of):
             value = jnp.dot(rows_of(0), grad[:, mine], preferred_element_type=F32)
@@ -462,12 +483,12 @@
             def emit_swapped():
                 arrive(("p", i), grad_m.at[:, got_cols])
 
-            op(("p", i), emit_swap, 0.02, -1 + rank, send=[(pair_link, 1024 * w, ("p", i))])
+            op(("p", i), emit_swap, 0.02, -10 + 0.01 * info["turn"], send=[(pair_link, 1024 * w, ("p", i))])
             op(("pr", i), emit_swapped, 0.01, rank, recv=[("p", i)], after=[f"g{m}t"])
             start = [("pr", i)]
 
         if kind == "A":
-            a_sum = bufs[f"a_sum{i}"]
+            a_sum, x_s, x_r = (bufs[f"{k}{i}"] for k in ("a_sum", "x_s", "x_r"))
 
             def emit_cross():
                 for u, j in enumerate((cross["y"], opposite)):
@@ -479,9 +500,19 @@
                 for u, j in enumerate((y, partner["y"])):
                     value = formed(lambda t: hid_t[t, j].reshape(ROWS, ROWS)) + x_r[u].astype(F32)
                     a_sum[u] = value.reshape(NZ, 64, w)
+                f_s[0] = a_sum[1, z].astype(BF16)
+                send(("f", i, 0), f_s.at[0], f_r.at[0], partner)
 
             op(("q", i), emit_cross, cost(1024), rank, send=[(cross_link, 2048 * w, ("q", i))], after=start)
-            op(("qf", i), emit_kept, cost(1024), rank, recv=[("q", i)], after=start)
+            op(
+                ("qf", i),
+                emit_kept,
+                cost(1024),
+                rank,
+                recv=[("q", i)],
+                send=[(pair_link, 128 * w, ("f", i, 0))],
+                after=start,
+            )
             start = [("qf", i)]
 
         def z_part(k, lo, count):
@@ -507,61 +538,69 @@
                 else:
                     arrive(("z", i, d, step - 1), z_r.at[d, step - 3])
                     z_s[d, step - 2] = (z_part(dest, 0, n) + z_r[d, step - 3].astype(F32)).astype(BF16)
-                send(("z", i, d, step), src, dst, toward("z", d))
+                if kind == "A" and step == 4:
+                    send(("z", i, d, 4), src.at[0], dst.at[0], toward("z", d))
+                    send(("f", i, 1 + d), src.at[1], f_r.at[1 + d], {**partner, **toward("z", d)})
+                else:
+                    send(("z", i, d, step), src, dst, toward("z", d))
 
             time = 0.012 if kind == "A" else cost(128 if step == 1 else 256)
+            alone = kind == "A" and step == 4
             op(
                 ("z", i, d, step),
                 emit,
                 time,
-                rank + (0.5 if step == 1 else 0),
+                rank + (FIRST if step == 1 else 0),
                 recv=[("z", i, d, step - 1)] if step > 1 else [],
-                send=[(links["z", d], 128 * w * (h if step == 1 else n), ("z", i, d, step))],
+                send=[(links["z", d], 128 * w * (1 if alone else h if step == 1 else n), ("z", i, d, step))]
+                + ([(links["z", d], 128 * w, ("f", i, 1 + d))] if alone else []),
                 after=start,
             )
 
         def emit_z_last():
+            if kind == "A":
+                for d in range(2):
+                    arrive(("z", i, d, 4), z_r.at[d, 2, 0])
+                gh_out[:, mine] = a_sum[0, z] + z_r[0, 2, 0].astype(F32) + z_r[1, 2, 0].astype(F32)
+                return
+            z_sum = bufs[f"z_sum{i}"]
             for d in range(2):
                 arrive(("z", i, d, 4), z_r.at[d, 2])
             z_sum[...] = z_part(0, 0, n) + z_r[0, 2].astype(F32) + z_r[1, 2].astype(F32)
-
-        def finish(kept, other):
-            f_s[...] = other.astype(BF16)
-            send(("f", i), f_s, f_r, partner)
-            if paired:
-                gh_out[:, mine] = kept
+            for u, device in enumerate((partner, cross, {"y": opposite})):
+                f_s[u] = z_sum[device["y"]].astype(BF16)
+                send(("f", i, u), f_s.at[u], f_r.at[u], device)
+
+        def emit_last():
+            for u in range(3):
+                arrive(("f", i, u), f_r.at[u])
+            got = [f_r[u].astype(F32) for u in range(3)]
+            if kind == "A":
+                gh_out[:, theirs] = got[0] + got[1] + got[2]
+            elif paired:
+                gh_out[:, mine] = bufs[f"z_sum{i}"][y] + got[1]
+                gh_out[:, theirs] = got[0] + got[2]
             else:
-                z_sum[0] = kept
-
-        def emit_last():
-            arrive(("f", i), f_r)
-            if paired:
-                gh_out[:, theirs] = f_r[...].astype(F32)
-            else:
-                gh_out[:, mine] = z_sum[0] + f_r[...].astype(F32)
+                gh_out[:, mine] = bufs[f"z_sum{i}"][y] + got[0] + got[1] + got[2]
 
         for d in range(2):
             for step in range(1, 5):
                 z_step(d, step)
-        op(("zf", i), emit_z_last, 0.012 if kind == "A" else cost(256), rank, recv=[("z", i, d, 4) for d in range(2)], after=start)
-        final = [(pair_link, 128 * w, ("f", i))]
-        if kind == "A":
-            op(("fs", i), lambda: finish(z_sum[0], z_sum[1]), 0.02, rank, send=final, after=[("zf", i)])
-            op(("ff", i), emit_last, 0.02, rank, recv=[("f", i)], after=[("fs", i)])
-        else:
-
-            def emit_cross_small():
-                for u, j in enumerate((cross["y"], opposite)):
-                    x_s[u] = z_sum[j].astype(BF16)
-                send(("q", i), x_s, x_r, cross)
-
-            def emit_kept_small():
-                arrive(("q", i), x_r)
-                finish(z_sum[y] + x_r[0].astype(F32), z_sum[partner["y"]] + x_r[1].astype(F32))
-
-            op(("q", i), emit_cross_small, 0.02, rank, send=[(cross_link, 256 * w, ("q", i))], after=[("zf", i)])
-            op(("qf", i), emit_kept_small, 0.02, rank, recv=[("q", i)], send=final, after=[("q", i)])
-            op(("ff", i), emit_last, 0.02, rank, recv=[("f", i)], after=[("qf", i)])
+        final = [] if kind == "A" else [
+            (pair_link, 128 * w, ("f", i, 0)),
+            (cross_link, 128 * w, ("f", i, 1)),
+            (cross_link, 256 * w, ("f", i, 2)),
+        ]
+        op(
+            ("zf", i),
+            emit_z_last,
+            0.012 if kind == "A" else cost(256),
+            rank,
+            recv=[("z", i, d, 4) for d in range(2)],
+            send=final,
+            after=start,
+        )
+        op(("ff", i), emit_last, 0.02, rank, recv=[("f", i, u) for u in range(3)], after=[("zf", i)])
 
     for i in range(len(TABLE)):
         chunk(i)
@@ -580,7 +619,7 @@
                 bufs["hs_s"][n, halves[h], :] = back(slot, h).astype(BF16)
             send(("hs", n), bufs["hs_s"].at[n], bufs["hs_r"].at[n], to_sib)
 
-        op(("hs", n), emit, 0.76, 3, send=[("c", 262144, ("hs", n))])
+        op(("hs", n), emit, 0.76, 30, send=[("c", 262144, ("hs", n))])
 
     def hg_step(n):
         def emit():
@@ -616,29 +655,11 @@
             2: [("x-", 262144, ("h2", 1))],
             3: [],
         }[n]
-        op(("hg", n), emit, 0.77 if n else 1.45, 3, recv=recv, send=sends)
+        op(("hg", n), emit, 0.77 if n else 1.45, 30, recv=recv, send=sends)
 
     for n in range(4):
         hs_step(n)
         hg_step(n)
-
-    def cross_share():
-        def emit():
-            def terms(rows):
-                total = None
-                for i in range(0, VOCAB, LANES):
-                    cols = slice(i, i + LANES)
-                    term = tea_exp[rows, cols] * (tea[rows, cols].astype(F32) - stu[rows, cols])
-                    total = term if total is None else total + term
-                part_b[rows, :] = total
-
-            row_blocks(16, terms)
-            ref = bufs["x_cross"]
-            ref[me, 4:8, :] = jnp.zeros((4, LANES), F32)
-            compact(ref, me, 0, None)
-            share("x_cross")
-
-        op("cross", emit, 1.06, 4)
 
     def divergence():
         def emit():
@@ -652,9 +673,8 @@
                 cross = term if cross is None else cross + term
             kl_out[...] = cross / total - peak - jnp.log(total) + s_peak + jnp.log(s_total)
 
-        op("kl", emit, 0.05, 5, after=["cross", ("hg", 3)])
-
-    cross_share()
+        op("kl", emit, 0.05, 40, after=[("hg", 3)])
+
     divergence()
 
     order, _ = in_order(ops)

time: 85.5 us -> 81.9 us (0.958); the launches traced: 84 us -> 81.7 us
  Pallas kernels: 83.4 us -> 81 us
    pallas_call x1, Pallas kernels: 81.4 us -> 79 us  [per_device(): pl.pallas_call(kernel, out_shape=(jax.ShapeDtypeStruct((4, LANES), F32),...]
where the time goes in v4:
time: 81.9 us; the launch traced here: 81.7 us
  Pallas kernels  81 us (99%)
    pallas_call x1, Pallas kernels, per_device(): pl.pallas_call(kernel, out_shape=(jax.ShapeDtypeStruct((4, LANES), F32),...  79 us
    pallas_call x1, Pallas kernels, per_device(): pl.pallas_call(handed_on, out_shape=tuple((jax.ShapeDtypeStruct(v.shape,...  2.03 us

profile of v4, /device:TPU:2, one launch (start us, length us, event | category | flops | bytes accessed | tf_op | source)
XLA Modules:
  0.0 81.7 jit_solution(17162671115897374174)
XLA Ops:
  0.6 79.0 %shard_map.58 = (f32[4,128]{1,0:T(4,128)}, bf16[512,256]{1,0:T(8,128)(2,1)}, f32[64,2048]{1,0:T(8,128)}) custom-call(bf16[512,256]{1,0:T(8,128)(2,1)} %hidden_in.1, bf16[512,2048]{1,0:T(8,128)(2,1)} %teacher_in.1, bf16[2048,2048]{1,0:T(8,128)(2,1)} %head_in.1), custom_call_target="tpu_custom_call" | custom-call | tf_op jit(solution)/shard_map/pallas_call | solution.py:696
  79.7 2.0 %shard_map.59 = (f32[4,128]{1,0:T(4,128)}, bf16[512,256]{1,0:T(8,128)(2,1)}, f32[64,2048]{1,0:T(8,128)}) custom-call(f32[4,128]{1,0:T(4,128)} %get-tuple-element.9.refs_0_, bf16[512,256]{1,0:T(8,128)(2,1)} %get-tuple-element.10.refs_1_, f32[64,2048]{1,0:T(8,128)} %get-tuple-element.11.refs_2_), custom_call_target="tpu_custom_call" | custom-call | tf_op jit(solution)/shard_map/pallas_call | solution.py:715

commit v5 on v4

--- a/solution.py
+++ b/solution.py
@@ -685,20 +685,15 @@
         copy.wait_send()
 
 
-def handed_on(*refs):
-    for src, dst in zip(refs[:3], refs[3:]):
-        dst[...] = src[...]
-
-
 def per_device(hidden_states, teacher_logits, head_weight):
     vmem = pl.BlockSpec(memory_space=pltpu.VMEM)
     hbm = pl.BlockSpec(memory_space=pl.ANY)
     kl, hidden_grad, head_grad = pl.pallas_call(
         kernel,
         out_shape=(
-            jax.ShapeDtypeStruct((4, LANES), F32),
-            jax.ShapeDtypeStruct((ROWS, PART), BF16),
-            jax.ShapeDtypeStruct((64, VOCAB), F32),
+            pltpu.VMEM((4, LANES), F32),
+            pltpu.VMEM((ROWS, PART), BF16),
+            pltpu.VMEM((64, VOCAB), F32),
         ),
         in_specs=[hbm, hbm, hbm],
         out_specs=(vmem, vmem, vmem),
@@ -709,15 +704,9 @@
             pltpu.SemaphoreType.DMA((N_COPIES,)),
         ],
         compiler_params=pltpu.CompilerParams(
-            collective_id=0, has_side_effects=True, vmem_limit_bytes=66_000_000
+            collective_id=0, has_side_effects=True, vmem_limit_bytes=64_500_000
         ),
     )(hidden_states, teacher_logits, head_weight)
-    kl, hidden_grad, head_grad = pl.pallas_call(
-        handed_on,
-        out_shape=tuple(jax.ShapeDtypeStruct(v.shape, v.dtype) for v in (kl, hidden_grad, head_grad)),
-        in_specs=[vmem] * 3,
-        out_specs=(vmem,) * 3,
-    )(kl, hidden_grad, head_grad)
     return kl.reshape(ROWS), hidden_grad, head_grad
 
 

time: 81.9 us -> 81.1 us (level)
  Pallas kernels: 81 us -> 78.2 us
  local copies, waits for them, and re-layouts: 0 us -> 2.08 us
    pallas_call x2 -> x1, Pallas kernels: 81 us -> 78.2 us  [per_device(): pl.pallas_call(kernel, out_shape=(pltpu.VMEM((4, LANES), F32), pltpu.VMEM...]
    unnamed x0 -> x3, local copies, waits for them, and re-layouts: none -> 2.08 us
where the time goes in v5:
time: 81.1 us; the launch traced here: 80.9 us
  Pallas kernels  78.2 us (96%)
  local copies, waits for them, and re-layouts  2.08 us (3%)
    pallas_call x1, Pallas kernels, per_device(): pl.pallas_call(kernel, out_shape=(pltpu.VMEM((4, LANES), F32), pltpu.VMEM...  78.2 us
    unnamed x3, local copies, waits for them, and re-layouts  2.08 us

profile of v5, /device:TPU:2, one launch (start us, length us, event | category | flops | bytes accessed | tf_op | source)
XLA Modules:
  0.0 80.9 jit_solution(12600897162440630674)
XLA Ops:
  0.6 78.2 %shard_map.58 = (f32[4,128]{1,0:T(4,128)S(1)}, bf16[512,256]{1,0:T(8,128)(2,1)S(1)}, f32[64,2048]{1,0:T(8,128)S(1)}) custom-call(bf16[512,256]{1,0:T(8,128)(2,1)} %hidden_in.1, bf16[512,2048]{1,0:T(8,128)(2,1)} %teacher_in.1, bf16[2048,2048]{1,0:T(8,128)(2,1)} %head_in.1), custom_call_target="tpu_custom_call" | custom-call | tf_op jit(solution)/shard_map/pallas_call | solution.py:691
  78.8 0.6 copy.9
  79.4 0.7 copy.10
  80.1 0.8 copy.11

commit v6 on v5

--- a/solution.py
+++ b/solution.py
@@ -17,6 +17,7 @@
 RANKS = (0.8, 6.2, 8.9, 2.0, 9.1, 6.0, 6.7, 2.5, 8.9, 6.5)
 SWAPS = (1, 2, 9, 3, 7, 6, 5, 4, 0, 8)
 FIRST = -3
+SWAP_FIRST = (0, 1, 8, 9)
 
 
 def chunk_table():
@@ -114,7 +115,7 @@
         SCRATCH[f"z_sum{_i}"] = ((4, 64, _w), F32)
 NAMES = tuple(SCRATCH)
 N_COPIES = 230
-WIDE = 1024
+WIDE = 2048
 
 
 def kernel(hidden_in, teacher_in, head_in, kl_out, hg_out, gh_out, *rest):
@@ -401,13 +402,11 @@
     stu_peak, stu_total = merged(bufs["x_stu"])
     spread(GRAD_SCALE * jnp.exp(bufs["x_stu"][me, 0:4, :] - stu_peak) / stu_total, part_a)
 
-    def grads(rows):
+    def grads(rows, begins):
         stu_scale, tea_scale = part_a[rows, :], part_b[rows, :]
-        for i in range(0, VOCAB, LANES):
+        for i in begins:
             cols = slice(i, i + LANES)
             grad[rows, cols] = (stu_exp[rows, cols] * stu_scale - tea_exp[rows, cols] * tea_scale).astype(BF16)
-
-    row_blocks(16, grads)
 
     ops = []
 
@@ -678,8 +677,17 @@
     divergence()
 
     order, _ = in_order(ops)
+    swaps = [step for step in order if step["name"][0] == "p"]
+    early = [step for step in swaps if step["name"][1] in SWAP_FIRST]
+    ranges = [(TABLE[i]["at"], TABLE[i]["at"] + 2 * TABLE[i]["w"]) for i in SWAP_FIRST]
+    tiles = [[b for b in range(0, VOCAB, LANES) if any(lo <= b < hi for lo, hi in ranges) == first] for first in (True, False)]
+    row_blocks(16, lambda rows: grads(rows, tiles[0]))
+    for step in early:
+        step["emit"]()
+    row_blocks(16, lambda rows: grads(rows, tiles[1]))
     for step in order:
-        step["emit"]()
+        if step not in early:
+            step["emit"]()
 
     for copy in sent:
         copy.wait_send()

time: 81.1 us -> 80.8 us (level)
  no operation moved by 1% of the time
where the time goes in v6:
time: 80.8 us; the launch traced here: 80.5 us
  Pallas kernels  77.8 us (96%)
  local copies, waits for them, and re-layouts  2.08 us (3%)
    pallas_call x1, Pallas kernels, per_device(): pl.pallas_call(kernel, out_shape=(pltpu.VMEM((4, LANES), F32), pltpu.VMEM...  77.8 us
    unnamed x3, local copies, waits for them, and re-layouts  2.08 us

profile of v6, /device:TPU:2, one launch (start us, length us, event | category | flops | bytes accessed | tf_op | source)
XLA Modules:
  0.0 80.5 jit_solution(16572735686866954897)
XLA Ops:
  0.6 77.8 %shard_map.58 = (f32[4,128]{1,0:T(4,128)S(1)}, bf16[512,256]{1,0:T(8,128)(2,1)S(1)}, f32[64,2048]{1,0:T(8,128)S(1)}) custom-call(bf16[512,256]{1,0:T(8,128)(2,1)} %hidden_in.1, bf16[512,2048]{1,0:T(8,128)(2,1)} %teacher_in.1, bf16[2048,2048]{1,0:T(8,128)(2,1)} %head_in.1), custom_call_target="tpu_custom_call" | custom-call | tf_op jit(solution)/shard_map/pallas_call | solution.py:699
  78.4 0.6 copy.9
  79.0 0.7 copy.10
  79.7 0.8 copy.11
